TPU v7x, 8 devices: a whole 2x2x1 slice. The times are simulated.
8 devices in a mesh: w: 4 (over z, y, x), h: 2 (over core).
Axes of the slice: x: 2, y: 2, z: 1, core: 2. Of those that a mesh axis runs over, the one named last changes fastest.
Arguments:
- x: bfloat16 [1, 64, 1024, 256], P(None, 'h', 'w')
- w1: bfloat16 [3, 3, 256, 256], replicated
- gamma: float32 [256], replicated
- beta: float32 [256], replicated
- w2: bfloat16 [3, 3, 256, 256], replicated
- g: bfloat16 [1, 64, 1024, 256], P(None, 'h', 'w')
Outputs:
- output 1: bfloat16 [1, 64, 1024, 256], P(None, 'h', 'w')
- output 2: bfloat16 [1, 64, 1024, 256], P(None, 'h', 'w')
- output 3: float32 [3, 3, 256, 256], replicated
- output 4: float32 [3, 3, 256, 256], replicated
- output 5: float32 [256], replicated
- output 6: float32 [256], replicated
All inputs are finite; a program needn't handle non-finite values.
Results may differ from a plain program's by a relative error of at most 0.00124822.
Values are sent between devices in bfloat16 or wider.
A program may use at most 1 GiB of HBM per device.

v0:
```python
import jax
import jax.numpy as jnp
from jax import lax
from jax.sharding import PartitionSpec as P

GROUPS = 32
EPS = 1e-5
DN = ('NHWC', 'HWIO', 'NHWC')


def _conv(up, w):
    return lax.conv_general_dilated(up, w, (1, 1), 'VALID', dimension_numbers=DN, preferred_element_type=jnp.float32)


def _flip_t(w):
    return jnp.flip(w, (0, 1)).transpose(0, 1, 3, 2)


def _wgrad(up, v):
    th, tw = v.shape[1], v.shape[2]
    return jnp.stack([jnp.stack([jnp.einsum('bhwc,bhwo->co', up[:, a:a + th, b:b + tw], v, preferred_element_type=jnp.float32) for b in range(3)]) for a in range(3)])


def _edge(u, axis, name, n):
    lo = lax.slice_in_dim(u, 0, 1, axis=axis)
    hi = lax.slice_in_dim(u, u.shape[axis] - 1, u.shape[axis], axis=axis)
    if n == 1:
        prev = jnp.zeros_like(lo)
        nxt = jnp.zeros_like(lo)
    else:
        prev = lax.ppermute(hi, name, [(i, i + 1) for i in range(n - 1)])
        nxt = lax.ppermute(lo, name, [(i + 1, i) for i in range(n - 1)])
    return jnp.concatenate([prev, u, nxt], axis=axis)


def solution(mesh):
    nh, nw = mesh.shape['h'], mesh.shape['w']
    tile = P(None, 'h', 'w', None)

    def halo(u):
        return _edge(_edge(u, 1, 'h', nh), 2, 'w', nw)

    def body(x, w1, gamma, beta, w2, g):
        nb, th, tw, c = x.shape
        cg = c // GROUPS
        cnt = th * nh * tw * nw * cg
        xp = halo(x)
        a = _conv(xp, w1).astype(jnp.bfloat16).astype(jnp.float32)
        s = jnp.stack([a.sum((1, 2)), (a * a).sum((1, 2))])
        s = lax.psum(s.reshape(2, nb, GROUPS, cg).sum(-1), ('h', 'w')) / cnt
        rstd_g = lax.rsqrt(s[1] - s[0] * s[0] + EPS)
        mean = jnp.repeat(s[0], cg, axis=-1)[:, None, None, :]
        rstd = jnp.repeat(rstd_g, cg, axis=-1)[:, None, None, :]
        xhatv = (a - mean) * rstd
        zf, gelu_vjp = jax.vjp(lambda n: jax.nn.gelu(n, approximate=True), xhatv * gamma + beta)
        z = zf.astype(jnp.bfloat16)
        zp = halo(z)
        y = (_conv(zp, w2) + x.astype(jnp.float32)).astype(jnp.bfloat16)
        gp = halo(g)
        dz = _conv(gp, _flip_t(w2))
        dw2 = lax.psum(_wgrad(zp, g), ('h', 'w'))
        (dn,) = gelu_vjp(dz)
        t = lax.psum(jnp.stack([(dn * xhatv).sum((1, 2)), dn.sum((1, 2))]), ('h', 'w'))
        dgamma = t[0].sum(0)
        dbeta = t[1].sum(0)
        u = jnp.repeat((t * gamma).reshape(2, nb, GROUPS, cg).sum(-1) / cnt, cg, axis=-1)[:, :, None, None, :]
        da = (rstd * (dn * gamma - u[1] - xhatv * u[0])).astype(jnp.bfloat16)
        dap = halo(da)
        dx = (_conv(dap, _flip_t(w1)) + g.astype(jnp.float32)).astype(jnp.bfloat16)
        dw1 = lax.psum(_wgrad(xp, da), ('h', 'w'))
        return y, dx, dw1, dw2, dgamma, dbeta

    return jax.shard_map(body, mesh=mesh, in_specs=(tile, P(), P(), P(), P(), tile), out_specs=(tile, tile, P(), P(), P(), P()), check_vma=False)
```

profile of v0, /device:TPU:0, one launch (start us, length us, event | category | flops | bytes accessed | tf_op | source)
XLA Modules:
  0.0 549.6 jit_solution(5828851175510749027)
XLA Ops:
  7.2 6.5 %copy.52 = bf16[1,32,256,256]{2,3,1,0:T(8,128)(2,1)} copy(bf16[1,32,256,256]{3,2,1,0:T(8,128)(2,1)} %param.6) | data formatting | bytes 8388608 | tf_op args[0]
  14.7 2.8 collective-permute-start
  20.5 3.7 collective-permute-start.8
  26.1 2.5 pad_maximum_fusion.2
  31.1 2.8 copy.55
  33.9 4.8 collective-permute-start.2
  46.8 5.2 collective-permute-start.10
  55.3 2.6 copy.58
  57.9 9.1 %maximum_bitcast_fusion = bf16[34,1,258,256]{2,3,0,1:T(8,128)(2,1)} fusion(bf16[1,34,1,256]{2,3,1,0:T(8,128)(2,1)} %copy.58, bf16[1,1,256,256]{2,3,1,0:T(8,128)(2,1)} %copy-done.20, bf16[1,32,256,256]{2,3,1,0:T(8,128)(2,1)} %copy.52, bf16[1,1,256,256]{2,3,1,0:T(8,128)(2,1)S(1)} %collective-permute-done, bf16[1,34,1,256]{2,3,1,0:T(8,128)(2,1)S(1)} %copy.57), kind=kLoop, calls=%fused_computation.42 | loop fusion | flops 22456320 | bytes 8982528 | tf_op jit(solution)/shard_map/concatenate | solution.py:33
  67.0 8.4 %copy.106 = bf16[34,1,258,256]{3,2,0,1:T(8,128)(2,1)} copy(bf16[34,1,258,256]{2,3,0,1:T(8,128)(2,1)} %maximum_bitcast_fusion) | data formatting | bytes 8982528
  75.4 4.7 pad.clone
  80.1 8.0 %reshape.184 = bf16[34,1,8,33,256]{4,3,2,0,1:T(8,128)(2,1)} reshape(bf16[34,1,264,256]{3,2,0,1:T(8,128)(2,1)} %pad.clone) | data formatting | bytes 9191424 | tf_op jit(solution)/shard_map/conv_general_dilated | solution.py:12
  88.1 3.9 copy.61
  92.1 13.1 %fusion.10 = (f32[256]{0:T(256)}, f32[256]{0:T(256)}, bf16[32,8,33,256]{3,1,2,0:T(8,128)(2,1)}) fusion(pred[8,33]{0,1:T(8,128)(4,1)S(1)} %copy-done.51, bf16[3,3,256,256]{3,2,1,0:T(8,128)(2,1)S(1)} %copy-done, bf16[34,1,7,2,256]{4,2,3,0,1:T(8,128)(2,1)S(1)} %slice.200, bf16[34,1,8,33,256]{4,2,3,0,1:T(8,128)(2,1)S(1)} %copy.61), kind=kOutput, calls=%fused_computation.16 | convolution fusion | flops 9997590528 | bytes 10346760 | tf_op jit(solution)/shard_map/conv_general_dilated | solution.py:12
  108.8 24.6 %psum.28 = f32[2,1,32]{2,0,1:T(2,128)S(1)} all-reduce(f32[2,1,32]{2,0,1:T(2,128)S(1)} %bitcast.339), channel_id=1, replica_groups=mesh['w'=4,'h'=2] {'h','w'}, use_global_device_ids=true, to_apply=%region_3.0 | all-reduce | flops 64 | bytes 512 | tf_op jit(solution)/shard_map/psum | solution.py:50
  136.0 3.6 maximum_bitcast_fusion.2
  139.6 2.5 pad.4
  142.1 8.0 %reshape.202 = bf16[34,1,8,33,256]{4,3,2,0,1:T(8,128)(2,1)} reshape(bf16[34,1,264,256]{3,2,0,1:T(8,128)(2,1)} %pad.4) | data formatting | bytes 9191424 | tf_op jit(solution)/shard_map/conv_general_dilated | solution.py:12
  150.1 4.0 copy.80
  154.2 21.7 %fusion.27 = (f32[256]{0:T(256)S(1)}, f32[256]{0:T(256)S(1)}, f32[32,8,33,256]{3,1,2,0:T(8,128)}) fusion(bf16[32,8,33,256]{3,1,2,0:T(8,128)(2,1)} %get-tuple-element.50, f32[256]{0:T(256)S(1)} %copy-done.47, f32[256]{0:T(256)S(1)} %copy-done.46, pred[8,33]{0,1:T(8,128)(4,1)S(1)} %copy-done.52, f32[256]{0:T(256)S(1)} %copy-done.48, f32[256]{0:T(256)S(1)} %copy-done.45, ...), kind=kOutput, calls=%fused_computation.33 | convolution fusion | flops 10045169664 | bytes 19001608 | tf_op jit(solution)/shard_map/conv_general_dilated | solution.py:12
  176.0 24.2 %psum.29 = f32[2,1,256]{2,0,1:T(2,128)S(1)} all-reduce(f32[2,1,256]{2,0,1:T(2,128)S(1)} %pad_maximum_fusion.13), channel_id=1, replica_groups=mesh['w'=4,'h'=2] {'h','w'}, use_global_device_ids=true, to_apply=%region_6.7 | all-reduce | flops 512 | bytes 4096 | tf_op jit(solution)/shard_map/psum | solution.py:63
  204.5 8.3 %fusion.25 = (bf16[32,8,33,256]{3,1,2,0:T(8,128)(2,1)S(1)}, bf16[32,8,33,256]{3,1,2,0:T(8,128)(2,1)S(1)}) fusion(bf16[32,8,33,256]{3,1,2,0:T(8,128)(2,1)} %get-tuple-element.50, f32[32,8,33,256]{3,1,2,0:T(8,128)} %get-tuple-element.51, f32[256]{0:T(256)} %broadcast_in_dim.28, f32[256]{0:T(256)} %broadcast_in_dim.30, f32[256]{0:T(256)} %param.8, ...), kind=kLoop, calls=%fused_computation.31 | loop fusion | flops 43253760 | bytes 21633024 | tf_op jit(solution)/shard_map/convert_element_type | solution.py:67
  218.7 8.0 %maximum_maximum_fusion = (bf16[1,34,257,256]{2,3,1,0:T(8,128)(2,1)}, bf16[1,34,257,256]{2,3,1,0:T(8,128)(2,1)}) fusion(bf16[1,1,256,256]{2,3,1,0:T(8,128)(2,1)S(1)} %copy-done.21, bf16[1,32,256,256]{2,3,1,0:T(8,128)(2,1)S(1)} %copy-done.1, bf16[1,1,256,256]{2,3,1,0:T(8,128)(2,1)S(1)} %collective-permute-done, bf16[1,34,1,256]{2,3,1,0:T(8,128)(2,1)S(1)} %copy.57, ...), kind=kLoop, calls=%fused_computation.44 | loop fusion | flops 35790848 | bytes 13438976 | tf_op jit(solution)/shard_map/concatenate | solution.py:33
  226.7 7.2 %fusion.132 = f32[1,256,256]{2,1,0:T(8,128)S(1)} fusion(bf16[1,34,257,256]{2,3,1,0:T(8,128)(2,1)} %get-tuple-element.26, bf16[32,1,256,256]{3,0,2,1:T(8,128)(2,1)S(1)} %slice.215), kind=kOutput, calls=%fused_computation.148 | convolution fusion | flops 1073741824 | bytes 8650752 | tf_op jit(solution)/shard_map/bhwc,bhwo->co/dot_general | solution.py:21
  233.9 5.0 fusion.143
  238.9 5.7 %fusion.140 = f32[1,256,256]{2,1,0:T(8,128)S(1)} fusion(bf16[1,34,257,256]{2,3,1,0:T(8,128)(2,1)S(1)} %bitcast.338, bf16[32,1,256,256]{3,0,2,1:T(8,128)(2,1)S(1)} %slice.215), kind=kOutput, calls=%fused_computation.150 | convolution fusion | flops 1073741824 | bytes 8650752 | tf_op jit(solution)/shard_map/bhwc,bhwo->co/dot_general | solution.py:21
  244.6 5.5 %fusion.146 = f32[1,256,256]{2,1,0:T(8,128)S(1)} fusion(bf16[1,34,257,256]{2,3,1,0:T(8,128)(2,1)S(1)} %bitcast.338, bf16[32,1,256,256]{3,0,2,1:T(8,128)(2,1)S(1)} %slice.215), kind=kOutput, calls=%fused_computation.152 | convolution fusion | flops 1073741824 | bytes 8650752 | tf_op jit(solution)/shard_map/bhwc,bhwo->co/dot_general | solution.py:21
  250.2 5.6 %fusion.122 = f32[1,256,256]{2,1,0:T(8,128)S(1)} fusion(bf16[1,32,256,256]{3,2,1,0:T(8,128)(2,1)S(1)} %copy-done.14, bf16[32,1,256,256]{3,0,2,1:T(8,128)(2,1)S(1)} %slice.215), kind=kOutput, calls=%fused_computation.146 | convolution fusion | flops 1073741824 | bytes 8650752 | tf_op jit(solution)/shard_map/bhwc,bhwo->co/dot_general | solution.py:21
  255.8 5.7 %fusion.149 = f32[1,256,256]{2,1,0:T(8,128)} fusion(bf16[1,34,257,256]{2,3,1,0:T(8,128)(2,1)S(1)} %copy-done.16, bf16[32,1,256,256]{3,0,2,1:T(8,128)(2,1)S(1)} %slice.215), kind=kOutput, calls=%fused_computation.153 | convolution fusion | flops 1073741824 | bytes 8650752 | tf_op jit(solution)/shard_map/bhwc,bhwo->co/dot_general | solution.py:21
  261.5 6.3 %fusion.157 = f32[1,256,256]{2,1,0:T(8,128)} fusion(bf16[1,34,257,256]{2,3,1,0:T(8,128)(2,1)S(1)} %bitcast.338, bf16[32,1,256,256]{3,0,2,1:T(8,128)(2,1)S(1)} %slice.215), kind=kOutput, calls=%fused_computation.155 | convolution fusion | flops 1073741824 | bytes 8650752 | tf_op jit(solution)/shard_map/bhwc,bhwo->co/dot_general | solution.py:21
  267.9 4.4 copy.147
  275.3 7.6 %copy.103 = bf16[32,1,256,256]{2,3,0,1:T(8,128)(2,1)} copy(bf16[32,1,256,256]{3,0,2,1:T(8,128)(2,1)} %slice.203) | data formatting | bytes 8388608
  287.3 5.4 fusion.127
  293.6 3.7 collective-permute-start.12
  299.6 9.1 %fusion.152 = f32[1,256,256]{2,1,0:T(8,128)S(1)} fusion(bf16[1,1,256,256]{2,3,1,0:T(8,128)(2,1)S(1)} %copy-done.22, bf16[1,32,256,256]{2,3,1,0:T(8,128)(2,1)} %copy.52, bf16[32,1,256,256]{3,0,2,1:T(8,128)(2,1)} %copy-done.12), kind=kOutput, calls=%fused_computation.154 | convolution fusion | flops 1075838976 | bytes 8781824 | tf_op jit(solution)/shard_map/bhwc,bhwo->co/dot_general | solution.py:21
  308.8 5.0 fusion.135
  320.4 2.8 copy.70
  323.2 4.8 collective-permute-start.6
  332.6 5.2 collective-permute-start.14
  339.3 6.1 %fusion.163 = f32[1,256,256]{2,1,0:T(8,128)} fusion(bf16[1,32,256,256]{3,2,1,0:T(8,128)(2,1)} %param.11, bf16[1,32,256,256]{2,3,1,0:T(8,128)(2,1)} %bitcast.326, bf16[1,1,256,256]{2,3,1,0:T(8,128)(2,1)S(1)} %copy-done.24), kind=kOutput, calls=%fused_computation.157 | convolution fusion | flops 1075838976 | bytes 8781824 | tf_op jit(solution)/shard_map/bhwc,bhwo->co/dot_general | solution.py:21
  349.1 2.6 copy.73
  351.7 8.2 %maximum_maximum_fusion.1 = (bf16[1,34,257,256]{2,3,1,0:T(8,128)(2,1)S(1)}, bf16[1,34,257,256]{2,3,1,0:T(8,128)(2,1)S(1)}) fusion(bf16[1,1,256,256]{2,3,1,0:T(8,128)(2,1)} %copy-done.25, bf16[1,32,256,256]{2,3,1,0:T(8,128)(2,1)} %bitcast.327, bf16[1,1,256,256]{2,3,1,0:T(8,128)(2,1)S(1)} %copy-done.24, bf16[1,34,1,256]{2,3,1,0:T(8,128)(2,1)S(1)} %copy.72, ...), kind=kLoop, calls=%fused_computation.46 | loop fusion | flops 35790848 | bytes 13438976 | tf_op jit(solution)/shard_map/concatenate | solution.py:33
  363.8 2.5 fusion.168
  366.4 2.5 fusion.174
  370.8 2.5 fusion.185
  373.4 3.4 maximum_bitcast_fusion.3
  376.8 2.5 pad.6
  379.2 8.1 %reshape.215 = bf16[34,1,8,33,256]{4,3,2,0,1:T(8,128)(2,1)} reshape(bf16[34,1,264,256]{3,2,0,1:T(8,128)(2,1)} %pad.6) | data formatting | bytes 9191424 | tf_op jit(solution)/shard_map/conv_general_dilated | solution.py:12
  387.4 3.9 copy.86
  391.4 13.2 %broadcast_select_fusion = f32[32,8,33,256]{3,1,2,0:T(8,128)} fusion(pred[8,33]{0,1:T(8,128)(4,1)S(1)} %copy-done.53, bf16[3,3,256,256]{3,2,1,0:T(8,128)(2,1)S(1)} %copy-done, bf16[34,1,7,2,256]{4,2,3,0,1:T(8,128)(2,1)S(1)} %slice.218, bf16[34,1,8,33,256]{4,2,3,0,1:T(8,128)(2,1)S(1)} %copy.86), kind=kOutput, calls=%fused_computation.76 | convolution fusion | flops 9982451712 | bytes 14670088 | tf_op jit(solution)/shard_map/conv_general_dilated | solution.py:12
  404.5 6.4 %copy.87 = f32[32,8,33,256]{3,0,2,1:T(8,128)S(1)} copy(f32[32,8,33,256]{3,1,2,0:T(8,128)} %broadcast_select_fusion) | data formatting | bytes 17301504 | tf_op jit(solution)/shard_map/conv_general_dilated | solution.py:12
  410.9 9.1 %fusion.29 = bf16[1,32,256,256]{3,1,2,0:T(8,128)(2,1)S(1)} fusion(f32[32,1,264,256]{3,0,2,1:T(8,128)S(1)} %bitcast.333, bf16[1,32,256,256]{3,2,1,0:T(8,128)(2,1)S(1)} %copy-done.11), kind=kLoop, calls=%fused_computation.38 | loop fusion | flops 6291456 | bytes 16777216 | tf_op jit(solution)/shard_map/convert_element_type | solution.py:69
  420.0 4.5 copy.98
  424.5 7.3 %maximum_bitcast_fusion.1 = bf16[34,1,258,256]{2,3,0,1:T(8,128)(2,1)} fusion(bf16[1,34,1,256]{2,3,1,0:T(8,128)(2,1)S(1)} %copy-done.8, bf16[1,1,256,256]{2,3,1,0:T(8,128)(2,1)S(1)} %copy-done.27, bf16[1,32,256,256]{2,3,1,0:T(8,128)(2,1)S(1)} %bitcast.330, bf16[1,1,256,256]{2,3,1,0:T(8,128)(2,1)S(1)} %copy-done.24, bf16[1,34,1,256]{2,3,1,0:T(8,128)(2,1)S(1)} %copy.72), kind=kLoop, calls=%fused_computation.43 | loop fusion | flops 22456320 | bytes 8982528 | tf_op jit(solution)/shard_map/concatenate | solution.py:33
  431.8 8.4 %copy.107 = bf16[34,1,258,256]{3,2,0,1:T(8,128)(2,1)} copy(bf16[34,1,258,256]{2,3,0,1:T(8,128)(2,1)} %maximum_bitcast_fusion.1) | data formatting | bytes 8982528
  440.2 4.7 pad.2.clone
  444.8 8.0 %reshape.197 = bf16[34,1,8,33,256]{4,3,2,0,1:T(8,128)(2,1)} reshape(bf16[34,1,264,256]{3,2,0,1:T(8,128)(2,1)} %pad.2.clone) | data formatting | bytes 9191424 | tf_op jit(solution)/shard_map/conv_general_dilated | solution.py:12
  452.9 4.1 copy.76
  461.2 14.4 %broadcast_select_fusion.1 = f32[32,8,33,256]{3,1,2,0:T(8,128)} fusion(pred[8,33]{0,1:T(8,128)(4,1)S(1)} %copy-done.53, bf16[3,3,256,256]{3,2,1,0:T(8,128)(2,1)S(1)} %copy-done.50, bf16[34,1,7,2,256]{4,2,3,0,1:T(8,128)(2,1)S(1)} %slice.208, bf16[34,1,8,33,256]{4,2,3,0,1:T(8,128)(2,1)} %copy-done.17), kind=kOutput, calls=%fused_computation.77 | convolution fusion | flops 9982451712 | bytes 14670088 | tf_op jit(solution)/shard_map/conv_general_dilated | solution.py:12
  475.6 6.4 %copy.77 = f32[32,8,33,256]{3,0,2,1:T(8,128)S(1)} copy(f32[32,8,33,256]{3,1,2,0:T(8,128)} %broadcast_select_fusion.1) | data formatting | bytes 17301504 | tf_op jit(solution)/shard_map/conv_general_dilated | solution.py:12
  482.0 9.1 %fusion.31 = bf16[1,32,256,256]{3,1,2,0:T(8,128)(2,1)S(1)} fusion(f32[32,1,264,256]{3,0,2,1:T(8,128)S(1)} %bitcast.334, bf16[1,32,256,256]{3,2,1,0:T(8,128)(2,1)S(1)} %copy-done.15), kind=kLoop, calls=%fused_computation.41 | loop fusion | flops 6291456 | bytes 16777216 | tf_op jit(solution)/shard_map/convert_element_type | solution.py:58
  491.1 4.4 copy.97
  495.6 41.9 %all-reduce.3.cloned.1.call-done = (f32[3,3,256,256]{3,2,1,0:T(8,128)}, f32[3,3,256,256]{3,2,1,0:T(8,128)}) async-done(((f32[3,3,256,256]{3,2,1,0:T(8,128)}, f32[3,3,256,256]{3,2,1,0:T(8,128)}), (f32[3,3,256,256]{3,2,1,0:T(8,128)}, f32[3,3,256,256]{3,2,1,0:T(8,128)})) %all-reduce.3.cloned.1.call-update) | async-done | bytes 4718608 | tf_op jit(solution)/shard_map/psum | solution.py:70
  537.4 3.4 copy.152
  (212 shorter events, 74.8 us)
Async XLA Ops:
  7.2 84.9 %copy-start = (bf16[3,3,256,256]{3,2,1,0:T(8,128)(2,1)S(1)}, bf16[3,3,256,256]{3,2,1,0:T(8,128)(2,1)}, u32[]{:S(2)}) copy-start(bf16[3,3,256,256]{3,2,1,0:T(8,128)(2,1)} %param.7) | copy-start | bytes 3538948
  7.2 530.2 %all-reduce.3.cloned.1.call-start = ((), (), s32[]{:S(2)}) async-start(), calls=%async_computation | async-start | bytes 9437184 | tf_op jit(solution)/shard_map/psum | solution.py:70
  14.7 10.7 %collective-permute-start = (bf16[1,1,256,256]{2,3,1,0:T(8,128)(2,1)S(1)}, bf16[1,1,256,256]{2,3,1,0:T(8,128)(2,1)S(1)}, u32[]{:S(2)}, u32[]{:S(2)}) collective-permute-start(bf16[1,1,256,256]{2,3,1,0:T(8,128)(2,1)S(1)} %get-tuple-element.44), channel_id=1, source_target_pairs={{0,1},{2,3},{4,5},{6,7}} | collective-permute-start | bytes 393224 | tf_op jit(solution)/shard_map/ppermute | solution.py:31
  17.5 8.0 %collective-permute-start.1 = (bf16[1,1,256,256]{2,3,1,0:T(8,128)(2,1)S(1)}, bf16[1,1,256,256]{2,3,1,0:T(8,128)(2,1)S(1)}, u32[]{:S(2)}, u32[]{:S(2)}) collective-permute-start(bf16[1,1,256,256]{2,3,1,0:T(8,128)(2,1)S(1)} %get-tuple-element.45), channel_id=1, source_target_pairs={{1,0},{3,2},{5,4},{7,6}} | collective-permute-start | bytes 393224 | tf_op jit(solution)/shard_map/ppermute | solution.py:32
  20.5 21.2 %collective-permute-start.8 = (bf16[1,1,256,256]{3,2,1,0:T(8,128)(2,1)}, bf16[1,1,256,256]{3,2,1,0:T(8,128)(2,1)}, u32[]{:S(2)}, u32[]{:S(2)}) collective-permute-start(bf16[1,1,256,256]{3,2,1,0:T(8,128)(2,1)} %get-tuple-element.43), channel_id=1, source_target_pairs={{0,1},{2,3},{4,5},{6,7}} | collective-permute-start | bytes 393224 | tf_op jit(solution)/shard_map/ppermute | solution.py:31
  24.2 20.9 %collective-permute-start.9 = (bf16[1,1,256,256]{3,2,1,0:T(8,128)(2,1)}, bf16[1,1,256,256]{3,2,1,0:T(8,128)(2,1)}, u32[]{:S(2)}, u32[]{:S(2)}) collective-permute-start(bf16[1,1,256,256]{3,2,1,0:T(8,128)(2,1)} %get-tuple-element.42), channel_id=1, source_target_pairs={{1,0},{3,2},{5,4},{7,6}} | collective-permute-start | bytes 393224 | tf_op jit(solution)/shard_map/ppermute | solution.py:32
  33.9 19.6 %collective-permute-start.2 = (bf16[1,34,1,256]{3,1,2,0:T(8,128)(2,1)}, bf16[1,34,1,256]{3,1,2,0:T(8,128)(2,1)}, u32[]{:S(2)}, u32[]{:S(2)}) collective-permute-start(bf16[1,34,1,256]{3,1,2,0:T(8,128)(2,1)} %copy.55), channel_id=1, source_target_pairs={{0,2},{2,4},{4,6},{1,3},{3,5},{5,7}} | collective-permute-start | bytes 52232 | tf_op jit(solution)/shard_map/ppermute | solution.py:31
  40.4 14.9 %collective-permute-start.3 = (bf16[1,34,1,256]{3,1,2,0:T(8,128)(2,1)}, bf16[1,34,1,256]{3,1,2,0:T(8,128)(2,1)}, u32[]{:S(2)}, u32[]{:S(2)}) collective-permute-start(bf16[1,34,1,256]{3,1,2,0:T(8,128)(2,1)} %copy.56), channel_id=1, source_target_pairs={{2,0},{4,2},{6,4},{3,1},{5,3},{7,5}} | collective-permute-start | bytes 52232 | tf_op jit(solution)/shard_map/ppermute | solution.py:32
  46.0 7.5 %copy-start.18 = (bf16[1,34,256,256]{3,2,1,0:T(8,128)(2,1)}, bf16[1,34,256,256]{3,2,1,0:T(8,128)(2,1)S(1)}, u32[]{:S(2)}) copy-start(bf16[1,34,256,256]{3,2,1,0:T(8,128)(2,1)S(1)} %constant_dynamic-update-slice_fusion) | copy-start | bytes 13369348
  46.8 89.2 %collective-permute-start.10 = (bf16[1,34,1,256]{3,2,1,0:T(2,128)(2,1)}, bf16[1,34,1,256]{3,2,1,0:T(2,128)(2,1)}, u32[]{:S(2)}, u32[]{:S(2)}) collective-permute-start(bf16[1,34,1,256]{3,2,1,0:T(2,128)(2,1)} %get-tuple-element.30), channel_id=1, source_target_pairs={{0,2},{2,4},{4,6},{1,3},{3,5},{5,7}} | collective-permute-start | bytes 52232 | tf_op jit(solution)/shard_map/ppermute | solution.py:31
  52.0 84.1 %collective-permute-start.11 = (bf16[1,34,1,256]{3,2,1,0:T(2,128)(2,1)}, bf16[1,34,1,256]{3,2,1,0:T(2,128)(2,1)}, u32[]{:S(2)}, u32[]{:S(2)}) collective-permute-start(bf16[1,34,1,256]{3,2,1,0:T(2,128)(2,1)} %get-tuple-element.31), channel_id=1, source_target_pairs={{2,0},{4,2},{6,4},{3,1},{5,3},{7,5}} | collective-permute-start | bytes 52232 | tf_op jit(solution)/shard_map/ppermute | solution.py:32
  88.1 4.0 copy-start.51
  150.1 4.1 copy-start.45
  150.1 4.1 copy-start.46
  150.1 4.1 copy-start.47
  150.1 4.1 copy-start.48
  150.1 4.1 copy-start.49
  150.1 4.1 copy-start.52
  215.8 2.9 copy-start.7
  218.7 49.2 %copy-start.12 = (bf16[32,1,256,256]{3,0,2,1:T(8,128)(2,1)}, bf16[32,1,256,256]{3,0,2,1:T(8,128)(2,1)S(1)}, u32[]{:S(2)}) copy-start(bf16[32,1,256,256]{3,0,2,1:T(8,128)(2,1)S(1)} %slice.215) | copy-start | bytes 12582916
  226.6 7.2 %copy-start.16 = (bf16[1,34,257,256]{2,3,1,0:T(8,128)(2,1)S(1)}, bf16[1,34,257,256]{2,3,1,0:T(8,128)(2,1)}, u32[]{:S(2)}) copy-start(bf16[1,34,257,256]{2,3,1,0:T(8,128)(2,1)} %get-tuple-element.26) | copy-start | bytes 13421572
  226.6 12.2 %slice-start = ((s8[6684672]{0:T(1024)(128)(4,1)}), s8[4194304]{0:T(1024)(128)(4,1)S(1)}, s32[]{:S(2)}) async-start(s8[6684672]{0:T(1024)(128)(4,1)} %bitcast.337), calls=%async_computation.1 | async-start | bytes 8388608
  233.9 5.0 slice-start.1
  244.6 5.5 %copy-start.14 = (bf16[1,32,256,256]{3,2,1,0:T(8,128)(2,1)S(1)}, bf16[1,32,256,256]{3,2,1,0:T(8,128)(2,1)}, u32[]{:S(2)}) copy-start(bf16[1,32,256,256]{3,2,1,0:T(8,128)(2,1)} %param.6) | copy-start | bytes 12582916
  267.9 4.4 copy-start.44
  275.3 7.6 %copy-start.31 = (bf16[1,8,33,256]{3,1,2,0:T(8,128)(2,1)S(1)}, bf16[1,8,33,256]{3,1,2,0:T(8,128)(2,1)}, u32[]{:S(2)}) copy-start(bf16[1,8,33,256]{3,1,2,0:T(8,128)(2,1)} %get-tuple-element.53) | copy-start | bytes 405508
  275.3 9.7 %copy-start.30 = (bf16[1,8,33,256]{3,1,2,0:T(8,128)(2,1)S(1)}, bf16[1,8,33,256]{3,1,2,0:T(8,128)(2,1)}, u32[]{:S(2)}) copy-start(bf16[1,8,33,256]{3,1,2,0:T(8,128)(2,1)} %get-tuple-element.52) | copy-start | bytes 405508
  283.7 31.7 %collective-permute-start.4 = (bf16[1,1,256,256]{2,3,1,0:T(8,128)(2,1)}, bf16[1,1,256,256]{2,3,1,0:T(8,128)(2,1)S(1)}, u32[]{:S(2)}, u32[]{:S(2)}) collective-permute-start(bf16[1,1,256,256]{2,3,1,0:T(8,128)(2,1)} %copy.102), channel_id=1, source_target_pairs={{0,1},{2,3},{4,5},{6,7}} | collective-permute-start | bytes 393224 | tf_op jit(solution)/shard_map/ppermute | solution.py:31
  285.9 6.9 %copy-start.29 = (bf16[1,8,33,256]{3,1,2,0:T(8,128)(2,1)S(1)}, bf16[1,8,33,256]{3,1,2,0:T(8,128)(2,1)}, u32[]{:S(2)}) copy-start(bf16[1,8,33,256]{3,1,2,0:T(8,128)(2,1)} %get-tuple-element.38) | copy-start | bytes 405508
  285.9 11.3 %copy-start.28 = (bf16[1,8,33,256]{3,1,2,0:T(8,128)(2,1)S(1)}, bf16[1,8,33,256]{3,1,2,0:T(8,128)(2,1)}, u32[]{:S(2)}) copy-start(bf16[1,8,33,256]{3,1,2,0:T(8,128)(2,1)} %get-tuple-element.39) | copy-start | bytes 405508
  285.9 13.7 %copy-start.22 = (bf16[1,1,256,256]{2,3,1,0:T(8,128)(2,1)S(1)}, bf16[1,1,256,256]{2,3,1,0:T(8,128)(2,1)}, u32[]{:S(2)}) copy-start(bf16[1,1,256,256]{2,3,1,0:T(8,128)(2,1)} %copy-done.20) | copy-start | bytes 393220
  285.9 29.6 %collective-permute-start.5 = (bf16[1,1,256,256]{2,3,1,0:T(8,128)(2,1)}, bf16[1,1,256,256]{2,3,1,0:T(8,128)(2,1)S(1)}, u32[]{:S(2)}, u32[]{:S(2)}) collective-permute-start(bf16[1,1,256,256]{2,3,1,0:T(8,128)(2,1)} %copy.104), channel_id=1, source_target_pairs={{1,0},{3,2},{5,4},{7,6}} | collective-permute-start | bytes 393224 | tf_op jit(solution)/shard_map/ppermute | solution.py:32
  293.6 37.3 %collective-permute-start.12 = (bf16[1,1,256,256]{3,2,1,0:T(8,128)(2,1)}, bf16[1,1,256,256]{3,2,1,0:T(8,128)(2,1)}, u32[]{:S(2)}, u32[]{:S(2)}) collective-permute-start(bf16[1,1,256,256]{3,2,1,0:T(8,128)(2,1)} %slice.214), channel_id=1, source_target_pairs={{0,1},{2,3},{4,5},{6,7}} | collective-permute-start | bytes 393224 | tf_op jit(solution)/shard_map/ppermute | solution.py:31
  298.0 10.7 %copy-start.35 = (f32[1,256,256]{2,1,0:T(8,128)S(1)}, f32[1,256,256]{2,1,0:T(8,128)}, u32[]{:S(2)}) copy-start(f32[1,256,256]{2,1,0:T(8,128)} %fusion.149) | copy-start | bytes 786436
  298.0 10.7 %copy-start.36 = (f32[1,256,256]{2,1,0:T(8,128)S(1)}, f32[1,256,256]{2,1,0:T(8,128)}, u32[]{:S(2)}) copy-start(f32[1,256,256]{2,1,0:T(8,128)} %fusion.157) | copy-start | bytes 786436
  298.0 10.8 %copy-start.2 = (bf16[1,32,256,256]{2,3,1,0:T(8,128)(2,1)S(1)}, bf16[1,32,256,256]{2,3,1,0:T(8,128)(2,1)}, u32[]{:S(2)}) copy-start(bf16[1,32,256,256]{2,3,1,0:T(8,128)(2,1)} %copy.52) | copy-start | bytes 12582916
  298.0 10.8 %copy-start.13 = (bf16[32,1,256,256]{3,0,2,1:T(8,128)(2,1)S(1)}, bf16[32,1,256,256]{3,0,2,1:T(8,128)(2,1)}, u32[]{:S(2)}) copy-start(bf16[32,1,256,256]{3,0,2,1:T(8,128)(2,1)} %copy-done.12) | copy-start | bytes 12582916
  298.0 32.9 %collective-permute-start.13 = (bf16[1,1,256,256]{3,2,1,0:T(8,128)(2,1)}, bf16[1,1,256,256]{3,2,1,0:T(8,128)(2,1)}, u32[]{:S(2)}, u32[]{:S(2)}) collective-permute-start(bf16[1,1,256,256]{3,2,1,0:T(8,128)(2,1)} %slice.217), channel_id=1, source_target_pairs={{1,0},{3,2},{5,4},{7,6}} | collective-permute-start | bytes 393224 | tf_op jit(solution)/shard_map/ppermute | solution.py:32
  313.8 3.1 copy-start.3
  320.4 18.9 %copy-start.24 = (bf16[1,1,256,256]{2,3,1,0:T(8,128)(2,1)S(1)}, bf16[1,1,256,256]{2,3,1,0:T(8,128)(2,1)}, u32[]{:S(2)}) copy-start(bf16[1,1,256,256]{2,3,1,0:T(8,128)(2,1)} %copy-done.23) | copy-start | bytes 393220
  323.2 24.2 %collective-permute-start.6 = (bf16[1,34,1,256]{3,1,2,0:T(8,128)(2,1)}, bf16[1,34,1,256]{3,1,2,0:T(8,128)(2,1)}, u32[]{:S(2)}, u32[]{:S(2)}) collective-permute-start(bf16[1,34,1,256]{3,1,2,0:T(8,128)(2,1)} %copy.70), channel_id=1, source_target_pairs={{0,2},{2,4},{4,6},{1,3},{3,5},{5,7}} | collective-permute-start | bytes 52232 | tf_op jit(solution)/shard_map/ppermute | solution.py:31
  329.6 19.5 %collective-permute-start.7 = (bf16[1,34,1,256]{3,1,2,0:T(8,128)(2,1)}, bf16[1,34,1,256]{3,1,2,0:T(8,128)(2,1)}, u32[]{:S(2)}, u32[]{:S(2)}) collective-permute-start(bf16[1,34,1,256]{3,1,2,0:T(8,128)(2,1)} %copy.71), channel_id=1, source_target_pairs={{2,0},{4,2},{6,4},{3,1},{5,3},{7,5}} | collective-permute-start | bytes 52232 | tf_op jit(solution)/shard_map/ppermute | solution.py:32
  332.6 40.8 %collective-permute-start.14 = (bf16[1,34,1,256]{3,2,1,0:T(2,128)(2,1)}, bf16[1,34,1,256]{3,2,1,0:T(2,128)(2,1)}, u32[]{:S(2)}, u32[]{:S(2)}) collective-permute-start(bf16[1,34,1,256]{3,2,1,0:T(2,128)(2,1)} %get-tuple-element.28), channel_id=1, source_target_pairs={{0,2},{2,4},{4,6},{1,3},{3,5},{5,7}} | collective-permute-start | bytes 52232 | tf_op jit(solution)/shard_map/ppermute | solution.py:31
  337.7 7.6 %copy-start.4 = (bf16[32,1,256,256]{2,3,0,1:T(8,128)(2,1)S(1)}, bf16[32,1,256,256]{2,3,0,1:T(8,128)(2,1)}, u32[]{:S(2)}) copy-start(bf16[32,1,256,256]{2,3,0,1:T(8,128)(2,1)} %copy.103) | copy-start | bytes 12582916
  337.7 7.6 %copy-start.9 = (bf16[1,32,256,256]{3,2,1,0:T(8,128)(2,1)S(1)}, bf16[1,32,256,256]{3,2,1,0:T(8,128)(2,1)}, u32[]{:S(2)}) copy-start(bf16[1,32,256,256]{3,2,1,0:T(8,128)(2,1)} %param.11) | copy-start | bytes 12582916
  337.7 7.6 %copy-start.26 = (bf16[1,1,256,256]{2,3,1,0:T(8,128)(2,1)S(1)}, bf16[1,1,256,256]{2,3,1,0:T(8,128)(2,1)}, u32[]{:S(2)}) copy-start(bf16[1,1,256,256]{2,3,1,0:T(8,128)(2,1)} %copy-done.25) | copy-start | bytes 393220
  337.7 35.6 %collective-permute-start.15 = (bf16[1,34,1,256]{3,2,1,0:T(2,128)(2,1)}, bf16[1,34,1,256]{3,2,1,0:T(2,128)(2,1)}, u32[]{:S(2)}, u32[]{:S(2)}) collective-permute-start(bf16[1,34,1,256]{3,2,1,0:T(2,128)(2,1)} %get-tuple-element.29), channel_id=1, source_target_pairs={{2,0},{4,2},{6,4},{3,1},{5,3},{7,5}} | collective-permute-start | bytes 52232 | tf_op jit(solution)/shard_map/ppermute | solution.py:32
  351.7 8.2 %copy-start.10 = (bf16[1,32,256,256]{3,2,1,0:T(8,128)(2,1)S(1)}, bf16[1,32,256,256]{3,2,1,0:T(8,128)(2,1)}, u32[]{:S(2)}) copy-start(bf16[1,32,256,256]{3,2,1,0:T(8,128)(2,1)} %param.11) | copy-start | bytes 12582916
  387.4 4.0 copy-start.53
  404.5 6.4 %copy-start.11 = (bf16[1,32,256,256]{3,2,1,0:T(8,128)(2,1)S(1)}, bf16[1,32,256,256]{3,2,1,0:T(8,128)(2,1)}, u32[]{:S(2)}) copy-start(bf16[1,32,256,256]{3,2,1,0:T(8,128)(2,1)} %param.11) | copy-start | bytes 12582916
  420.0 4.5 copy-start.5
  420.0 4.5 copy-start.8
  420.0 4.5 copy-start.27
  452.8 6.4 %copy-start.34 = (f32[1,256,256]{2,1,0:T(8,128)S(1)}, f32[1,256,256]{2,1,0:T(8,128)}, u32[]{:S(2)}) copy-start(f32[1,256,256]{2,1,0:T(8,128)} %fusion.163) | copy-start | bytes 786436
  452.8 6.4 %copy-start.41 = (f32[1,256,256]{2,1,0:T(8,128)S(1)}, f32[1,256,256]{2,1,0:T(8,128)}, u32[]{:S(2)}) copy-start(f32[1,256,256]{2,1,0:T(8,128)} %fusion.160) | copy-start | bytes 786436
  452.8 6.4 %copy-start.42 = (f32[1,256,256]{2,1,0:T(8,128)S(1)}, f32[1,256,256]{2,1,0:T(8,128)}, u32[]{:S(2)}) copy-start(f32[1,256,256]{2,1,0:T(8,128)} %fusion.168) | copy-start | bytes 786436
  452.8 6.5 %copy-start.32 = (f32[1,256,256]{2,1,0:T(8,128)S(1)}, f32[1,256,256]{2,1,0:T(8,128)}, u32[]{:S(2)}) copy-start(f32[1,256,256]{2,1,0:T(8,128)} %fusion.127) | copy-start | bytes 786436
  452.8 6.5 %copy-start.37 = (f32[1,256,256]{2,1,0:T(8,128)S(1)}, f32[1,256,256]{2,1,0:T(8,128)}, u32[]{:S(2)}) copy-start(f32[1,256,256]{2,1,0:T(8,128)} %fusion.171) | copy-start | bytes 786436
  452.8 6.5 %copy-start.40 = (f32[1,256,256]{2,1,0:T(8,128)S(1)}, f32[1,256,256]{2,1,0:T(8,128)}, u32[]{:S(2)}) copy-start(f32[1,256,256]{2,1,0:T(8,128)} %fusion.174) | copy-start | bytes 786436
  452.9 6.5 %copy-start.33 = (f32[1,256,256]{2,1,0:T(8,128)S(1)}, f32[1,256,256]{2,1,0:T(8,128)}, u32[]{:S(2)}) copy-start(f32[1,256,256]{2,1,0:T(8,128)} %fusion.180) | copy-start | bytes 786436
  452.9 6.5 %copy-start.38 = (f32[1,256,256]{2,1,0:T(8,128)S(1)}, f32[1,256,256]{2,1,0:T(8,128)}, u32[]{:S(2)}) copy-start(f32[1,256,256]{2,1,0:T(8,128)} %fusion.177) | copy-start | bytes 786436
  452.9 6.5 %copy-start.39 = (f32[1,256,256]{2,1,0:T(8,128)S(1)}, f32[1,256,256]{2,1,0:T(8,128)}, u32[]{:S(2)}) copy-start(f32[1,256,256]{2,1,0:T(8,128)} %fusion.185) | copy-start | bytes 786436
  475.6 6.4 %copy-start.15 = (bf16[1,32,256,256]{3,2,1,0:T(8,128)(2,1)S(1)}, bf16[1,32,256,256]{3,2,1,0:T(8,128)(2,1)}, u32[]{:S(2)}) copy-start(bf16[1,32,256,256]{3,2,1,0:T(8,128)(2,1)} %param.6) | copy-start | bytes 12582916
  537.4 3.4 copy-start.19
  (9 other events, 15.6 us)
Sparse Core Ops, SparseCore 0:
  461.2 76.2 all-reduce.2
where the time goes:
time: 556 us; the launch traced here: 550 us
  local copies, waits for them, and re-layouts  180 us (32%)
  matrix products  144 us (26%)
  other arithmetic  76.8 us (14%)
  blocking collectives  48.8 us (9%)
  starting transfers between devices  42.5 us (8%)
  waiting for transfers between devices  41.9 us (8%)
  between operations  15.6 us (3%)
    dot_general x18, matrix products, _wgrad(): jnp.einsum('bhwc,bhwo->co', up[:, a:a + th, b:b + tw], v, preferred_eleme...  82 us
    conv_general_dilated x4, matrix products, _conv(): lax.conv_general_dilated(up, w, (1, 1), 'VALID', dimension_numbers=DN, pr...  62.4 us
    conv_general_dilated x14, local copies, waits for them, and re-layouts, _conv(): lax.conv_general_dilated(up, w, (1, 1), 'VALID', dimension_numbers=DN, pr...  61 us
    unnamed x125, local copies, waits for them, and re-layouts  60.9 us
    concatenate x8, other arithmetic, _edge(): return jnp.concatenate([prev, u, nxt], axis=axis)  43 us
    psum x1, waiting for transfers between devices, body(): dw1 = lax.psum(_wgrad(xp, da), ('h', 'w'))  41.9 us
    ppermute x8, starting transfers between devices, _edge(): prev = lax.ppermute(hi, name, [(i, i + 1) for i in range(n - 1)])  31.3 us
    psum x1, blocking collectives, body(): s = lax.psum(s.reshape(2, nb, GROUPS, cg).sum(-1), ('h', 'w')) / cnt  24.6 us
  transfers between devices with their start and end apart: 17, of which 1 were waited for; matrix products, arithmetic and copies ran while one was open for 32% of the time, Pallas kernels for 0%

commit v1 on v0

v1 whole, which is shorter than its diff:
```python
import functools

import jax
import jax.numpy as jnp
from jax import lax
from jax.experimental import pallas as pl
from jax.experimental.pallas import tpu as pltpu
from jax.sharding import PartitionSpec as P

GROUPS = 32
EPS = 1e-5
MESH = pl.DeviceIdType.MESH
F32 = jnp.float32
BF16 = jnp.bfloat16
GC0 = 0.7978845608028654
GC1 = 0.044715
TH, TW, C = 32, 256, 256
CG = C // GROUPS
NW, NH = 4, 2
ND = NW * NH
CNT = float(TH * NH * TW * NW * CG)
TB = 16
EXT = TW + 2 * TB
R = 4
NX = 4


def _group_sum(v):
    lane = lax.broadcasted_iota(jnp.int32, v.shape, 1)
    for k in (1, 2, 4):
        up = pltpu.roll(v, C - k, 1)
        down = pltpu.roll(v, k, 1)
        v = v + jnp.where((lane & k) == 0, up, down)
    return v


def _fold8(v):
    return v.reshape(v.shape[0] // 8, 8, C).sum(0)


def kernel(x_hbm, w1_hbm, gam_ref, bet_ref, w2_hbm, g_hbm,
           y_hbm, dx_hbm, dw1_hbm, dw2_hbm, dgam_ref, dbet_ref,
           xn, gn, ux, ug, uz, ud, abuf, dz, vt, w1, w2, w1t, w2t, dw, rd, r1, r2,
           cs, cr, cc, stat, pm, qm,
           in_sem, out_sem, hs_send, hs_recv, st_send, st_recv, ar_send, ar_recv):
    w = lax.axis_index("w")
    h = lax.axis_index("h")
    me = w * NH + h

    rows = TH // NX
    loads = {}
    for q, (src, dst) in enumerate(((x_hbm, xn), (g_hbm, gn))):
        for k in range(NX):
            cp = pltpu.make_async_copy(src.at[pl.ds(k * rows, rows)], dst.at[pl.ds(k * rows, rows)], in_sem.at[q * NX + k])
            cp.start()
            loads[q, k] = cp
        wsrc, wdst = ((w1_hbm, w1), (w2_hbm, w2))[q]
        cp = pltpu.make_async_copy(wsrc, wdst, in_sem.at[2 * NX + q])
        cp.start()
        loads[q, "w"] = cp

    barrier = pltpu.get_barrier_semaphore()
    for k in range(1, ND):
        t = lax.rem(me + k, ND)
        pl.semaphore_signal(barrier, inc=1, device_id={"w": t // NH, "h": lax.rem(t, NH)}, device_id_type=MESH)

    pi = lax.broadcasted_iota(jnp.int32, (EXT, TW), 0)
    pj = lax.broadcasted_iota(jnp.int32, (EXT, TW), 1)
    pm[...] = jnp.where(pj == (pi & 15) * TB + (pi >> 4) - 1, 1.0, 0.0).astype(BF16)
    qi = lax.broadcasted_iota(jnp.int32, (TW, TW), 0)
    qj = lax.broadcasted_iota(jnp.int32, (TW, TW), 1)
    qm[...] = jnp.where(qi == (qj & 15) * TB + (qj >> 4), 1.0, 0.0).astype(BF16)
    for u in (ux, ug, uz, ud):
        u[pl.ds(33 * h, 1)] = jnp.zeros((1, EXT, C), BF16)

    @pl.when(w == 0)
    def _():
        for q in range(4):
            cr[q, 0] = jnp.zeros((TH, C), F32)
            cc[q, 0] = jnp.zeros((8, C), F32)

    @pl.when(w == NW - 1)
    def _():
        for q in range(4):
            cr[q, 1] = jnp.zeros((TH, C), F32)
            cc[q, 1] = jnp.zeros((8, C), F32)

    def to_dev(dw_, dh):
        return {"w": w + dw_, "h": h if dh == 0 else 1 - h}

    def rcopy(src, dst, ss, rs, dev):
        return pltpu.make_async_remote_copy(src_ref=src, dst_ref=dst, send_sem=ss, recv_sem=rs, device_id=dev, device_id_type=MESH)

    def halo_copies(q, u):
        row = rcopy(u.at[pl.ds(32 - 31 * h, 1)], u.at[pl.ds(33 * h, 1)], hs_send.at[q, 0], hs_recv.at[q, 0], to_dev(0, 1))
        slab = pl.ds(pl.multiple_of(24 * (1 - h), 8), 8)
        left = [rcopy(cs.at[q, 0], cr.at[q, 1], hs_send.at[q, 1], hs_recv.at[q, 1], to_dev(-1, 0)),
                rcopy(cs.at[q, 0, slab], cc.at[q, 1], hs_send.at[q, 2], hs_recv.at[q, 2], to_dev(-1, 1))]
        right = [rcopy(cs.at[q, 1], cr.at[q, 0], hs_send.at[q, 3], hs_recv.at[q, 3], to_dev(1, 0)),
                 rcopy(cs.at[q, 1, slab], cc.at[q, 0], hs_send.at[q, 4], hs_recv.at[q, 4], to_dev(1, 1))]
        return row, left, right

    def halo_start(q, u):
        row, left, right = halo_copies(q, u)
        row.start()

        @pl.when(w > 0)
        def _():
            for cp in left:
                cp.start()

        @pl.when(w < NW - 1)
        def _():
            for cp in right:
                cp.start()

    sub = lax.broadcasted_iota(jnp.int32, (TB, C), 0)

    def put(u, r, lo, hi):
        b0 = u[r, 0:TB, :].astype(F32)
        u[r, 0:TB, :] = jnp.where(sub == 0, lo, b0).astype(BF16)
        b1 = u[r, TW + TB:EXT, :].astype(F32)
        u[r, TW + TB:EXT, :] = jnp.where(sub == TB - 1, hi, b1).astype(BF16)

    def halo_finish(q, u):
        row, left, right = halo_copies(q, u)
        row.wait()

        @pl.when(w > 0)
        def _():
            for cp in left:
                cp.wait_send()
            for cp in right:
                cp.wait_recv()

        @pl.when(w < NW - 1)
        def _():
            for cp in right:
                cp.wait_send()
            for cp in left:
                cp.wait_recv()

        def step(k, _):
            for i in range(4):
                r = k * 4 + i
                put(u, r + 1, cr[q, 0, pl.ds(r, 1), :], cr[q, 1, pl.ds(r, 1), :])
            return 0
        lax.fori_loop(0, TH // 4, step, 0)
        put(u, 33 * (1 - h), cc[q, 0, pl.ds(7 * h, 1), :], cc[q, 1, pl.ds(7 * h, 1), :])

    def permute_in(q, src, u):
        for k in range(NX):
            loads[q, k].wait()

            def step(i, _):
                for d in range(4):
                    r = k * rows + i * 4 + d
                    v = jnp.dot(pm[...], src[r], preferred_element_type=F32)
                    u[r + 1] = v.astype(BF16)
                    cs[q, 0, pl.ds(r, 1), :] = v[TB:TB + 1]
                    cs[q, 1, pl.ds(r, 1), :] = v[TW + TB - 1:TW + TB]
                return 0
            lax.fori_loop(0, rows // 4, step, 0)

    def pad_blocks(q, u, r, first, last):
        u[r + 1, 0:TB, :] = jnp.where(sub == 0, 0.0, pltpu.roll(last, 1, 0)).astype(BF16)
        u[r + 1, TW + TB:EXT, :] = jnp.where(sub == TB - 1, 0.0, pltpu.roll(first, TB - 1, 0)).astype(BF16)
        cs[q, 0, pl.ds(r, 1), :] = first[0:1]
        cs[q, 1, pl.ds(r, 1), :] = last[TB - 1:TB]

    def conv(u, wt, r0):
        lhs = jnp.concatenate([u[pl.ds(r0 + a, R), TB * b:TB * b + TW, :].reshape(R * TW, C) for a in range(3) for b in range(3)], axis=1)
        return jnp.dot(lhs, wt[...], preferred_element_type=F32)

    def stat_copies(q):
        out = []
        for k in range(1, ND):
            t = lax.rem(me + k, ND)
            out.append(rcopy(stat.at[q, me], stat.at[q, me], st_send.at[q, k], st_recv.at[q, me], {"w": t // NH, "h": lax.rem(t, NH)}))
        return out

    def stat_start(q, a, b):
        stat[q, me] = jnp.concatenate([a, b, jnp.zeros((6, C), F32)], axis=0)
        for cp in stat_copies(q):
            cp.start()

    def stat_finish(q):
        for k in range(1, ND):
            t = lax.rem(me + k, ND)
            rcopy(stat.at[q, t], stat.at[q, t], st_send.at[q, k], st_recv.at[q, t], {"w": t // NH, "h": lax.rem(t, NH)}).wait_recv()
        for cp in stat_copies(q):
            cp.wait_send()
        tot = stat[q, 0]
        for k in range(1, ND):
            tot = tot + stat[q, k]
        return tot

    xb = lax.rem(w, 2)
    yb = w // 2
    dev_x = {"w": w + 1 - 2 * xb, "h": h}
    dev_y = {"w": w + 2 - 4 * yb, "h": h}
    dev_c = {"w": w, "h": 1 - h}

    def part(n, off, size):
        return dw.at[n, :, pl.ds(pl.multiple_of(off, 16), size), :]

    def half(n, off, size):
        return rd.at[n, :, pl.ds(pl.multiple_of(off, 16), size), :]

    def ar_copies(n):
        mine, other = 128 * h, 128 * (1 - h)
        c = []
        s = [0]

        def add(src, dst, dev):
            k = s[0]
            c.append(lambda: rcopy(src, dst, ar_send.at[n, k], ar_recv.at[n, k], dev))
            s[0] += 1
        add(part(n, other, 128), rd.at[n], dev_c)
        add(part(n, mine + 32 * (1 - xb), 32), r1.at[n, 0], dev_x)
        add(part(n, mine + 64 + 32 * (1 - yb), 32), r1.at[n, 1], dev_y)
        add(part(n, mine + 32 * xb + 16 * (1 - yb), 16), r2.at[n, 0], dev_y)
        add(part(n, mine + 64 + 32 * yb + 16 * (1 - xb), 16), r2.at[n, 1], dev_x)
        o0, o1 = 32 * xb + 16 * yb, 64 + 32 * yb + 16 * xb
        add(half(n, o0, 16), half(n, o0, 16), dev_y)
        add(half(n, o1, 16), half(n, o1, 16), dev_x)
        add(half(n, 32 * xb, 32), half(n, 32 * xb, 32), dev_x)
        add(half(n, 64 + 32 * yb, 32), half(n, 64 + 32 * yb, 32), dev_y)
        out = (dw2_hbm, dw1_hbm)[n].at[:, pl.ds(pl.multiple_of(mine, 128), 128), :]
        add(rd.at[n], out, dev_c)
        c.append(lambda: pltpu.make_async_copy(rd.at[n], out, in_sem.at[n]))
        return c

    AR_SETS = ((0,), (1, 2), (3, 4), (5, 6), (7, 8), (9, 10))

    def accumulate(n, off, size, src, into=None):
        def step(t, _):
            sl = pl.ds(pl.multiple_of(128 * h + off, 16), size)
            v = dw[n, t, sl, :] + src[t]
            if into is None:
                dw[n, t, sl, :] = v
            else:
                rd[n, t, pl.ds(pl.multiple_of(off, 16), size), :] = v
            return 0
        lax.fori_loop(0, 9, step, 0)

    def ar_step(n, k):
        cps = ar_copies(n)
        if k > 0:
            for i in AR_SETS[k - 1]:
                cps[i]().wait()
        if k == 1:
            accumulate(n, 0, 128, rd.at[n])
        if k == 2:
            accumulate(n, 32 * xb, 32, r1.at[n, 0])
            accumulate(n, 64 + 32 * yb, 32, r1.at[n, 1])
        if k == 3:
            accumulate(n, 32 * xb + 16 * yb, 16, r2.at[n, 0], rd)
            accumulate(n, 64 + 32 * yb + 16 * xb, 16, r2.at[n, 1], rd)
        if k < 6:
            for i in AR_SETS[k]:
                cps[i]().start()

    def wgrad(n, u):
        def step(t, _):
            a = t // 3
            b = lax.rem(t, 3)
            rhs = u[pl.ds(a, TH), pl.ds(pl.multiple_of(TB * b, TB), TW), :].reshape(TH * TW, C)
            acc = jnp.dot(vt[...], rhs, preferred_element_type=F32)
            dw[n, t] = acc.T
            return 0
        lax.fori_loop(0, 9, step, 0)

    pl.semaphore_wait(barrier, ND - 1)
    permute_in(0, xn, ux)
    halo_start(0, ux)
    permute_in(1, gn, ug)
    halo_start(1, ug)
    loads[0, "w"].wait()
    loads[1, "w"].wait()

    def wtrans(t, _):
        w1t[pl.ds(pl.multiple_of((8 - t) * C, C), C), :] = w1[pl.ds(pl.multiple_of(t * C, C), C), :].T
        w2t[pl.ds(pl.multiple_of((8 - t) * C, C), C), :] = w2[pl.ds(pl.multiple_of(t * C, C), C), :].T
        return 0
    lax.fori_loop(0, 9, wtrans, 0)
    halo_finish(0, ux)

    def conv1_step(k, carry):
        s1, s2 = carry
        a = conv(ux, w1, k * R).astype(BF16)
        abuf[pl.ds(k * R, R)] = a.reshape(R, TW, C)
        af = a.astype(F32)
        return s1 + _fold8(af), s2 + _fold8(af * af)
    zero = jnp.zeros((8, C), F32)
    s1, s2 = lax.fori_loop(0, TH // R, conv1_step, (zero, zero))
    stat_start(0, s1.sum(0, keepdims=True), s2.sum(0, keepdims=True))
    halo_finish(1, ug)

    def convt2_step(k, _):
        dz[pl.ds(k * R, R)] = conv(ug, w2t, k * R).reshape(R, TW, C)
        for i in range(R):
            r = k * R + i
            vt[:, pl.ds(pl.multiple_of(r * TW, TW), TW)] = ug[r + 1, TB:TB + TW, :].T
        return 0
    lax.fori_loop(0, TH // R, convt2_step, 0)

    tot = _group_sum(stat_finish(0)) / CNT
    mean = tot[0:1]
    rstd = lax.rsqrt(tot[1:2] - mean * mean + EPS)
    gam = gam_ref[...]
    bet = bet_ref[...]

    SB = 32

    def act_step(r, carry):
        t0, t1 = carry
        first = last = None
        for i in range(TW // SB):
            p = i * SB
            xhat = (abuf[r, p:p + SB, :].astype(F32) - mean) * rstd
            n = xhat * gam + bet
            n2 = n * n
            th = jnp.tanh(GC0 * (n + GC1 * (n * n2)))
            hp = 0.5 + 0.5 * th
            z = n * hp
            dg = hp + (0.5 * GC0) * n * (1.0 - th * th) * (1.0 + (3.0 * GC1) * n2)
            dn = dz[r, p:p + SB, :] * dg
            dz[r, p:p + SB, :] = dn
            uz[r + 1, TB + p:TB + p + SB, :] = z.astype(BF16)
            t0 = t0 + _fold8(dn * xhat)
            t1 = t1 + _fold8(dn)
            if i == 0:
                first = z[0:TB]
            if i == TW // SB - 1:
                last = z[SB - TB:SB]
        pad_blocks(2, uz, r, first, last)
        return t0, t1
    t0, t1 = lax.fori_loop(0, TH, act_step, (zero, zero))
    stat_start(1, t0.sum(0, keepdims=True), t1.sum(0, keepdims=True))
    halo_start(2, uz)
    halo_finish(2, uz)
    wgrad(0, uz)
    ar_step(0, 0)

    tot = stat_finish(1)
    dgam_ref[...] = tot[0:1]
    dbet_ref[...] = tot[1:2]
    us = _group_sum(tot * gam) / CNT
    k0 = rstd * gam
    k1 = rstd * us[0:1]
    k2 = rstd * us[1:2]

    def da_step(r, _):
        first = last = None
        for i in range(TW // SB):
            p = i * SB
            xhat = (abuf[r, p:p + SB, :].astype(F32) - mean) * rstd
            d = dz[r, p:p + SB, :] * k0 - k2 - xhat * k1
            ud[r + 1, TB + p:TB + p + SB, :] = d.astype(BF16)
            if i == 0:
                first = d[0:TB]
            if i == TW // SB - 1:
                last = d[SB - TB:SB]
        pad_blocks(3, ud, r, first, last)
        vt[:, pl.ds(pl.multiple_of(r * TW, TW), TW)] = ud[r + 1, TB:TB + TW, :].T
        return 0
    lax.fori_loop(0, TH, da_step, 0)
    halo_start(3, ud)
    ar_step(0, 1)
    wgrad(1, ux)
    halo_finish(3, ud)
    ar_step(1, 0)
    ar_step(0, 2)

    def out_copy(q, k):
        src, dst = ((xn, y_hbm), (gn, dx_hbm))[q]
        return pltpu.make_async_copy(src.at[pl.ds(k * R, R)], dst.at[pl.ds(k * R, R)], out_sem.at[q, k])

    def out_step(q, u, wt, res, out, k):
        acc = conv(u, wt, k * R).reshape(R, TW, C)
        for i in range(R):
            r = k * R + i
            v = (acc[i] + res[r + 1, TB:TB + TW, :].astype(F32)).astype(BF16)
            out[r] = jnp.dot(qm[...], v, preferred_element_type=F32).astype(BF16)
        out_copy(q, k).start()

    def y_step(k, _):
        out_step(0, uz, w2, ux, xn, k)
        return 0

    def dx_step(k, _):
        out_step(1, ud, w1t, ug, gn, k)
        return 0
    hk = TH // R // 2
    lax.fori_loop(0, hk, y_step, 0)
    ar_step(0, 3)
    ar_step(1, 1)
    lax.fori_loop(hk, TH // R, y_step, 0)
    ar_step(0, 4)
    ar_step(1, 2)
    lax.fori_loop(0, hk, dx_step, 0)
    ar_step(0, 5)
    ar_step(1, 3)
    lax.fori_loop(hk, TH // R, dx_step, 0)
    ar_step(0, 6)
    ar_step(1, 4)
    ar_step(1, 5)
    ar_step(1, 6)
    for q in range(2):
        for k in range(TH // R):
            out_copy(q, k).wait()


def solution(mesh):
    tile = P(None, 'h', 'w', None)

    def body(x, w1, gamma, beta, w2, g):
        anyspec = pl.BlockSpec(memory_space=pl.ANY)
        vspec = pl.BlockSpec(memory_space=pltpu.VMEM)
        S = jax.ShapeDtypeStruct
        V = pltpu.VMEM
        DMA = pltpu.SemaphoreType.DMA
        img = (TH, TW, C)
        uimg = (TH + 2, EXT, C)
        y, dx, dw1, dw2, dgam, dbet = pl.pallas_call(
            kernel,
            out_shape=(S(img, BF16), S(img, BF16), S((9, C, C), F32), S((9, C, C), F32), S((1, C), F32), S((1, C), F32)),
            in_specs=[anyspec, anyspec, vspec, vspec, anyspec, anyspec],
            out_specs=(anyspec, anyspec, anyspec, anyspec, vspec, vspec),
            scratch_shapes=[
                V(img, BF16), V(img, BF16), V(uimg, BF16), V(uimg, BF16), V(uimg, BF16), V(uimg, BF16),
                V(img, BF16), V(img, F32), V((C, TH * TW), BF16),
                V((9 * C, C), BF16), V((9 * C, C), BF16), V((9 * C, C), BF16), V((9 * C, C), BF16),
                V((2, 9, C, C), F32), V((2, 9, 128, C), F32), V((2, 2, 9, 32, C), F32), V((2, 2, 9, 16, C), F32),
                V((4, 2, TH, C), F32), V((4, 2, TH, C), F32), V((4, 2, 8, C), F32), V((2, ND, 8, C), F32),
                V((EXT, TW), BF16), V((TW, TW), BF16),
                DMA((2 * NX + 2,)), DMA((2, TH // R)), DMA((4, 5)), DMA((4, 5)), DMA((2, ND)), DMA((2, ND)), DMA((2, 10)), DMA((2, 10)),
            ],
            compiler_params=pltpu.CompilerParams(collective_id=0, has_side_effects=True, vmem_limit_bytes=67043328),
        )(x.reshape(img), w1.reshape(9 * C, C), gamma.reshape(1, C), beta.reshape(1, C), w2.reshape(9 * C, C), g.reshape(img))
        return (y.reshape(x.shape), dx.reshape(x.shape), dw1.reshape(w1.shape), dw2.reshape(w2.shape), dgam.reshape(C), dbet.reshape(C))

    return jax.shard_map(body, mesh=mesh, in_specs=(tile, P(), P(), P(), P(), tile), out_specs=(tile, tile, P(), P(), P(), P()), check_vma=False)
```

time: 556 us -> 136 us (0.24); the launches traced: 550 us -> 135 us
  local copies, waits for them, and re-layouts: 180 us -> 13 us
  matrix products: 144 us -> 0 us
  Pallas kernels: 0 us -> 122 us
  other arithmetic: 76.8 us -> 0 us
  blocking collectives: 48.8 us -> 0 us
  starting transfers between devices: 42.5 us -> 0 us
  waiting for transfers between devices: 41.9 us -> 0 us
  between operations: 15.6 us -> 0.66 us
    pallas_call x0 -> x1, Pallas kernels: none -> 122 us  [body(): pl.pallas_call(kernel, out_shape=(S(img, BF16), S(img, BF16), S((9, C, C)...]
    dot_general x18 -> x0, matrix products: 82 us -> none  [_wgrad(): jnp.einsum('bhwc,bhwo->co', up[:, a:a + th, b:b + tw], v, preferred_eleme...]
    conv_general_dilated x4 -> x0, matrix products: 62.4 us -> none  [_conv(): lax.conv_general_dilated(up, w, (1, 1), 'VALID', dimension_numbers=DN, pr...]
    conv_general_dilated x14 -> x0, local copies, waits for them, and re-layouts: 61 us -> none  [_conv(): lax.conv_general_dilated(up, w, (1, 1), 'VALID', dimension_numbers=DN, pr...]
    psum x2 -> x0, blocking collectives: 48.8 us -> none  [the longest x1 24.6 us: body(): s = lax.psum(s.reshape(2, nb, GROUPS, cg).sum(-1), ('h', 'w')) / cnt]
    unnamed x125 -> x16, local copies, waits for them, and re-layouts: 60.9 us -> 13 us
    concatenate x8 -> x0, other arithmetic: 43 us -> none  [_edge(): return jnp.concatenate([prev, u, nxt], axis=axis)]
    ppermute x16 -> x0, starting transfers between devices: 42.4 us -> none  [the longest x8 31.3 us: _edge(): prev = lax.ppermute(hi, name, [(i, i + 1) for i in range(n - 1)])]
  transfers between devices with their start and end apart: 17 -> 0, of which waited for: 1 -> 0; matrix products, arithmetic and copies ran while one was open for 32% -> 0% of each run, Pallas kernels for 0% -> 0%
where the time goes in v1:
time: 136 us; the launch traced here: 135 us
  Pallas kernels  122 us (90%)
  local copies, waits for them, and re-layouts  13 us (10%)
    pallas_call x1, Pallas kernels, body(): pl.pallas_call(kernel, out_shape=(S(img, BF16), S(img, BF16), S((9, C, C)...  122 us
    unnamed x16, local copies, waits for them, and re-layouts  13 us

profile of v1, /device:TPU:0, one launch (start us, length us, event | category | flops | bytes accessed | tf_op | source)
XLA Modules:
  0.0 135.4 jit_solution(16736401061682575756)
XLA Ops:
  0.6 121.7 %shard_map.109 = (bf16[32,256,256]{2,1,0:T(8,128)(2,1)}, bf16[32,256,256]{2,1,0:T(8,128)(2,1)}, f32[9,256,256]{2,1,0:T(8,128)}, f32[9,256,256]{2,1,0:T(8,128)}, f32[1,256]{1,0:T(1,128)}, /*index=5*/f32[1,256]{1,0:T(1,128)}) custom-call(bf16[32,256,256]{2,1,0:T(8,128)(2,1)} %bitcast.12, bf16[2304,256]{1,0:T(8,128)(2,1)} %bitcast.18, f32[1,256]{1,0:T(1,128)} %bitcast.20, ...), custom_call_target="tpu_custom_call" | custom-call | tf_op jit(solution)/shard_map/pallas_call | solution.py:426
  122.4 0.0 copy-start
  122.4 4.8 %copy.18 = bf16[1,32,256,256]{3,2,1,0:T(8,128)(2,1)} copy(bf16[1,32,256,256]{3,2,1,0:T(8,128)(2,1)} %bitcast.15) | data formatting | bytes 8388608
  127.2 0.0 copy-done
  127.2 0.0 copy-start.2
  127.2 2.1 %copy.19 = bf16[1,32,256,256]{3,2,1,0:T(8,128)(2,1)} copy(bf16[1,32,256,256]{3,2,1,0:T(8,128)(2,1)S(1)} %bitcast.14) | data formatting | bytes 8388608
  129.3 1.0 copy-done.2
  130.3 0.0 copy-start.1
  130.3 0.0 copy-start.4
  130.3 0.0 copy-start.3
  130.3 1.4 %copy.20 = f32[3,3,256,256]{3,2,1,0:T(8,128)} copy(f32[3,3,256,256]{3,2,1,0:T(8,128)S(1)} %bitcast.17) | data formatting | bytes 4718592
  131.7 1.1 copy-done.1
  132.9 1.4 %copy.21 = f32[3,3,256,256]{3,2,1,0:T(8,128)} copy(f32[3,3,256,256]{3,2,1,0:T(8,128)S(1)} %bitcast.16) | data formatting | bytes 4718592
  134.3 0.0 copy-done.4
  134.3 0.6 copy.22
  134.8 0.0 copy-done.3
  134.8 0.6 copy.23
Async XLA Ops:
  122.4 4.8 %copy-start = (bf16[32,256,256]{2,1,0:T(8,128)(2,1)S(1)}, bf16[32,256,256]{2,1,0:T(8,128)(2,1)}, u32[]{:S(2)}) copy-start(bf16[32,256,256]{2,1,0:T(8,128)(2,1)} %get-tuple-element.13) | copy-start | bytes 12582916
  127.2 3.2 %copy-start.2 = (f32[9,256,256]{2,1,0:T(8,128)S(1)}, f32[9,256,256]{2,1,0:T(8,128)}, u32[]{:S(2)}) copy-start(f32[9,256,256]{2,1,0:T(8,128)} %get-tuple-element.14) | copy-start | bytes 7077892
  130.3 2.5 %copy-start.1 = (f32[9,256,256]{2,1,0:T(8,128)S(1)}, f32[9,256,256]{2,1,0:T(8,128)}, u32[]{:S(2)}) copy-start(f32[9,256,256]{2,1,0:T(8,128)} %get-tuple-element.15) | copy-start | bytes 7077892
  130.3 3.9 %copy-start.4 = (f32[1,256]{1,0:T(1,128)S(1)}, f32[1,256]{1,0:T(1,128)}, u32[]{:S(2)}) copy-start(f32[1,256]{1,0:T(1,128)} %get-tuple-element.16) | copy-start | bytes 3076
  130.3 4.5 %copy-start.3 = (f32[1,256]{1,0:T(1,128)S(1)}, f32[1,256]{1,0:T(1,128)}, u32[]{:S(2)}) copy-start(f32[1,256]{1,0:T(1,128)} %get-tuple-element.17) | copy-start | bytes 3076

commit v2 on v1

v2 whole, which is shorter than its diff:
```python
import functools

import jax
import jax.numpy as jnp
from jax import lax
from jax.experimental import pallas as pl
from jax.experimental.pallas import tpu as pltpu
from jax.sharding import PartitionSpec as P

GROUPS = 32
EPS = 1e-5
MESH = pl.DeviceIdType.MESH
F32 = jnp.float32
BF16 = jnp.bfloat16
GC0 = 0.7978845608028654
GC1 = 0.044715
TH, TW, C = 32, 256, 256
CG = C // GROUPS
NW, NH = 4, 2
ND = NW * NH
CNT = float(TH * NH * TW * NW * CG)
TB = 16
EXT = TW + 2 * TB
R = 4
NX = 2


def _group_sum(v):
    lane = lax.broadcasted_iota(jnp.int32, v.shape, 1)
    for k in (1, 2, 4):
        up = pltpu.roll(v, C - k, 1)
        down = pltpu.roll(v, k, 1)
        v = v + jnp.where((lane & k) == 0, up, down)
    return v


def _fold8(v):
    return v.reshape(v.shape[0] // 8, 8, C).sum(0)


def kernel(x_hbm, w1_hbm, gam_hbm, bet_hbm, w2_hbm, g_hbm,
           y_hbm, dx_hbm, dw1_hbm, dw2_hbm, dgam_hbm, dbet_hbm,
           xn, gn, ux, ug, uz, ud, abuf, ost, dz, raw, w1, w2, w1t, w2t, dw, rd, r1, r2,
           cs, cr, cc, stat, pm, vec,
           in_sem, vec_sem, out_sem, hs_send, hs_recv, st_send, st_recv, ar_send, ar_recv):
    w = lax.axis_index("w")
    h = lax.axis_index("h")
    me = w * NH + h

    rows = TH // NX
    loads = {}
    for q, (src, dst) in enumerate(((x_hbm, xn), (g_hbm, gn))):
        for k in range(NX):
            cp = pltpu.make_async_copy(src.at[pl.ds(k * rows, rows)], dst.at[pl.ds(k * rows, rows)], in_sem.at[q * NX + k])
            cp.start()
            loads[q, k] = cp
        wsrc, wdst = ((w1_hbm, w1), (w2_hbm, w2))[q]
        cp = pltpu.make_async_copy(wsrc, wdst, in_sem.at[2 * NX + q])
        cp.start()
        loads[q, "w"] = cp
        cp = pltpu.make_async_copy((gam_hbm, bet_hbm)[q], vec.at[q], vec_sem.at[q])
        cp.start()
        loads[q, "v"] = cp

    barrier = pltpu.get_barrier_semaphore()
    for k in range(1, ND):
        t = lax.rem(me + k, ND)
        pl.semaphore_signal(barrier, inc=1, device_id={"w": t // NH, "h": lax.rem(t, NH)}, device_id_type=MESH)

    pi = lax.broadcasted_iota(jnp.int32, (EXT, TW), 0)
    pj = lax.broadcasted_iota(jnp.int32, (EXT, TW), 1)
    pm[...] = jnp.where(pj == (pi & 15) * TB + (pi >> 4) - 1, 1.0, 0.0).astype(BF16)
    for u in (ux, ug, uz, ud):
        u[pl.ds(33 * h, 1)] = jnp.zeros((1, EXT, C), BF16)

    @pl.when(w == 0)
    def _():
        for q in range(4):
            cr[q, 0] = jnp.zeros((TH, C), F32)
            cc[q, 0] = jnp.zeros((8, C), F32)

    @pl.when(w == NW - 1)
    def _():
        for q in range(4):
            cr[q, 1] = jnp.zeros((TH, C), F32)
            cc[q, 1] = jnp.zeros((8, C), F32)

    def to_dev(dw_, dh):
        return {"w": w + dw_, "h": h if dh == 0 else 1 - h}

    def rcopy(src, dst, ss, rs, dev):
        return pltpu.make_async_remote_copy(src_ref=src, dst_ref=dst, send_sem=ss, recv_sem=rs, device_id=dev, device_id_type=MESH)

    def halo_copies(q, u):
        slab = pl.ds(pl.multiple_of(24 * (1 - h), 8), 8)

        def make(m, src, dst, dev):
            return lambda: rcopy(src, dst, hs_send.at[q, m], hs_recv.at[q, m], dev)
        row = make(0, u.at[pl.ds(32 - 31 * h, 1)], u.at[pl.ds(33 * h, 1)], to_dev(0, 1))
        left = [make(1, cs.at[q, 0], cr.at[q, 1], to_dev(-1, 0)), make(2, cs.at[q, 0, slab], cc.at[q, 1], to_dev(-1, 1))]
        right = [make(3, cs.at[q, 1], cr.at[q, 0], to_dev(1, 0)), make(4, cs.at[q, 1, slab], cc.at[q, 0], to_dev(1, 1))]
        return row, left, right

    def halo_start(q, u):
        row, left, right = halo_copies(q, u)
        row().start()

        @pl.when(w > 0)
        def _():
            for cp in left:
                cp().start()

        @pl.when(w < NW - 1)
        def _():
            for cp in right:
                cp().start()

    sub = lax.broadcasted_iota(jnp.int32, (TB, C), 0)

    def put(u, r, lo, hi):
        b0 = u[r, 0:TB, :].astype(F32)
        u[r, 0:TB, :] = jnp.where(sub == 0, lo, b0).astype(BF16)
        b1 = u[r, TW + TB:EXT, :].astype(F32)
        u[r, TW + TB:EXT, :] = jnp.where(sub == TB - 1, hi, b1).astype(BF16)

    def halo_row(q, u):
        halo_copies(q, u)[0]().wait()

    def halo_cols(q, u):
        _, left, right = halo_copies(q, u)

        @pl.when(w > 0)
        def _():
            for cp in left:
                cp().wait_send()
            for cp in right:
                cp().wait_recv()

        @pl.when(w < NW - 1)
        def _():
            for cp in right:
                cp().wait_send()
            for cp in left:
                cp().wait_recv()

        def step(k, _):
            for i in range(4):
                r = k * 4 + i
                put(u, r + 1, cr[q, 0, pl.ds(r, 1), :], cr[q, 1, pl.ds(r, 1), :])
            return 0
        lax.fori_loop(0, TH // 4, step, 0)
        put(u, 33 * (1 - h), cc[q, 0, pl.ds(7 * h, 1), :], cc[q, 1, pl.ds(7 * h, 1), :])

    def permute_in(q, src, u):
        for k in range(NX):
            loads[q, k].wait()

            def step(i, _):
                for d in range(16):
                    r = k * rows + i * 16 + d
                    v = jnp.dot(pm[...], src[r], preferred_element_type=F32)
                    u[r + 1] = v.astype(BF16)
                    cs[q, 0, pl.ds(r, 1), :] = v[TB:TB + 1]
                    cs[q, 1, pl.ds(r, 1), :] = v[TW + TB - 1:TW + TB]
                return 0
            lax.fori_loop(0, rows // 16, step, 0)

    def pad_blocks(q, u, r, first, last):
        u[r + 1, 0:TB, :] = jnp.where(sub == 0, 0.0, pltpu.roll(last, 1, 0)).astype(BF16)
        u[r + 1, TW + TB:EXT, :] = jnp.where(sub == TB - 1, 0.0, pltpu.roll(first, TB - 1, 0)).astype(BF16)
        cs[q, 0, pl.ds(r, 1), :] = first[0:1]
        cs[q, 1, pl.ds(r, 1), :] = last[TB - 1:TB]

    def conv(u, wt, r0, R=R):
        lhs = jnp.concatenate([u[pl.ds(r0 + a, R), TB * b:TB * b + TW, :].reshape(R * TW, C) for a in range(3) for b in range(3)], axis=1)
        return jnp.dot(lhs, wt[...], preferred_element_type=F32)

    def stat_copies(q):
        out = []
        for k in range(1, ND):
            t = lax.rem(me + k, ND)
            out.append(rcopy(stat.at[q, me], stat.at[q, me], st_send.at[q, k], st_recv.at[q, me], {"w": t // NH, "h": lax.rem(t, NH)}))
        return out

    def stat_start(q, a, b):
        stat[q, me] = jnp.concatenate([a, b, jnp.zeros((6, C), F32)], axis=0)
        for cp in stat_copies(q):
            cp.start()

    def stat_finish(q):
        for k in range(1, ND):
            t = lax.rem(me + k, ND)
            rcopy(stat.at[q, t], stat.at[q, t], st_send.at[q, k], st_recv.at[q, t], {"w": t // NH, "h": lax.rem(t, NH)}).wait_recv()
        for cp in stat_copies(q):
            cp.wait_send()
        tot = stat[q, 0]
        for k in range(1, ND):
            tot = tot + stat[q, k]
        return tot

    xb = lax.rem(w, 2)
    yb = w // 2
    dev_x = {"w": w + 1 - 2 * xb, "h": h}
    dev_y = {"w": w + 2 - 4 * yb, "h": h}
    dev_c = {"w": w, "h": 1 - h}

    BS = (1, 0, 2)

    def part(n, c, off, size):
        return dw.at[n, c, :, pl.ds(pl.multiple_of(off, 16), size), :]

    def half(n, c, off, size):
        return rd.at[n, c, :, pl.ds(pl.multiple_of(off, 16), size), :]

    def ar_copies(n, c):
        mine, other = 128 * h, 128 * (1 - h)
        o0, o1 = 32 * xb + 16 * yb, 64 + 32 * yb + 16 * xb
        q0, q1 = 32 * xb, 64 + 32 * yb
        out = (dw2_hbm, dw1_hbm)[n].at[:, BS[c], pl.ds(pl.multiple_of(mine, 128), 128), :]
        plan = (
            (part(n, c, other, 128), rd.at[n, c], dev_c),
            (part(n, c, mine + 32 * (1 - xb), 32), r1.at[n, c, 0], dev_x),
            (part(n, c, mine + 64 + 32 * (1 - yb), 32), r1.at[n, c, 1], dev_y),
            (part(n, c, mine + 32 * xb + 16 * (1 - yb), 16), r2.at[n, c, 0], dev_y),
            (part(n, c, mine + 64 + 32 * yb + 16 * (1 - xb), 16), r2.at[n, c, 1], dev_x),
            (half(n, c, o0, 16), half(n, c, o0, 16), dev_y),
            (half(n, c, o1, 16), half(n, c, o1, 16), dev_x),
            (half(n, c, q0, 32), half(n, c, q0, 32), dev_x),
            (half(n, c, q1, 32), half(n, c, q1, 32), dev_y),
            (rd.at[n, c], out, dev_c),
        )

        def make(k):
            src, dst, dev = plan[k]
            return lambda: rcopy(src, dst, ar_send.at[n, c, k], ar_recv.at[n, c, k], dev)
        return [make(k) for k in range(10)] + [lambda: pltpu.make_async_copy(rd.at[n, c], out, in_sem.at[n * 3 + c])]

    AR_SETS = ((0,), (1, 2), (3, 4), (5, 6), (7, 8), (9, 10))

    def accumulate(n, c, off, size, src, into=None):
        sl = pl.ds(pl.multiple_of(128 * h + off, 16), size)
        for t in range(3):
            v = dw[n, c, t, sl, :] + src[t]
            if into is None:
                dw[n, c, t, sl, :] = v
            else:
                rd[n, c, t, pl.ds(pl.multiple_of(off, 16), size), :] = v

    def ar_step(n, c, k):
        with jax.named_scope(f"ar_{n}_{c}_{k}"):
            cps = ar_copies(n, c)
            if k > 0:
                for i in AR_SETS[k - 1]:
                    cps[i]().wait()
            if k == 1:
                accumulate(n, c, 0, 128, rd.at[n, c])
            if k == 2:
                accumulate(n, c, 32 * xb, 32, r1.at[n, c, 0])
                accumulate(n, c, 64 + 32 * yb, 32, r1.at[n, c, 1])
            if k == 3:
                accumulate(n, c, 32 * xb + 16 * yb, 16, r2.at[n, c, 0], rd)
                accumulate(n, c, 64 + 32 * yb + 16 * xb, 16, r2.at[n, c, 1], rd)
            if k < 6:
                for i in AR_SETS[k]:
                    cps[i]().start()

    LAG = (0, 1, 5, 9, 12, 16, 18)
    START = (4, 7, 9, 13, 16, 18)
    SLOTS = {(i // 3, i % 3): [min(s_ + l_, 34) for l_ in LAG] for i, s_ in enumerate(START)}
    plan_at = {}
    for (n_, c_), at_ in SLOTS.items():
        for k_, s_ in enumerate(at_):
            plan_at.setdefault(s_, []).append((n_, c_, k_))

    def sums_at(base, lo, hi, i):
        for sl in range(lo, hi):
            if sl + base in plan_at:
                def _(todo=plan_at[sl + base]):
                    for n, c, k in sorted(todo, key=lambda e: -e[2]):
                        ar_step(n, c, k)
                pl.when(i == sl)(_)

    def perm3(i):
        return (3 * i * i - 5 * i + 2) // 2

    def turn(n, t):
        dw[n, t // 3, perm3(lax.rem(t, 3))] = raw[...].T

    def tap(n, u, vt, t):
        turn(n, lax.max(t - 1, 0))
        a = perm3(lax.rem(t, 3))
        b = perm3(t // 3)
        rhs = u[pl.ds(a, TH), pl.ds(pl.multiple_of(TB * b, TB), TW), :].reshape(TH * TW, C)
        lhs = jnp.concatenate([vt[r] for r in range(TH)], axis=1)
        raw[...] = jnp.dot(lhs, rhs, preferred_element_type=F32)

    with jax.named_scope("barrier"):
        pl.semaphore_wait(barrier, ND - 1)
    with jax.named_scope("perm_x"):
        permute_in(0, xn, ux)
    with jax.named_scope("hstart"):
        halo_start(0, ux)
    with jax.named_scope("perm_g"):
        permute_in(1, gn, ug)
    with jax.named_scope("hstart"):
        halo_start(1, ug)
    loads[0, "w"].wait()
    loads[1, "w"].wait()

    def wtrans(t, _):
        w1t[pl.ds(pl.multiple_of((8 - t) * C, C), C), :] = w1[pl.ds(pl.multiple_of(t * C, C), C), :].T
        w2t[pl.ds(pl.multiple_of((8 - t) * C, C), C), :] = w2[pl.ds(pl.multiple_of(t * C, C), C), :].T
        return 0
    with jax.named_scope("wtrans"):
        lax.fori_loop(0, 9, wtrans, 0)
    with jax.named_scope("hfin_x"):
        halo_row(0, ux)
        halo_cols(0, ux)

    def conv1_step(k, carry):
        s1, s2 = carry
        a = conv(ux, w1, k * 8, 8).astype(BF16)
        abuf[pl.ds(k * 8, 8)] = a.reshape(8, TW, C)
        af = a.astype(F32)
        return s1 + _fold8(af), s2 + _fold8(af * af)
    zero = jnp.zeros((8, C), F32)
    with jax.named_scope("conv1"):
        s1, s2 = lax.fori_loop(0, TH // 8, conv1_step, (zero, zero))
    with jax.named_scope("ststart"):
        stat_start(0, s1.sum(0, keepdims=True), s2.sum(0, keepdims=True))
    with jax.named_scope("hfin_g"):
        halo_row(1, ug)
        halo_cols(1, ug)

    def convt2(k):
        dz[pl.ds(k * R, R)] = conv(ug, w2t, k * R).reshape(R, TW, C)
        for i in range(R):
            r = k * R + i
            gn[r] = ug[r + 1, TB:TB + TW, :].T

    def convt2_first(k, _):
        convt2(k)
        return 0
    with jax.named_scope("convt2"):
        lax.fori_loop(0, 4, convt2_first, 0)

    with jax.named_scope("stat0"):
        tot = _group_sum(stat_finish(0)) / CNT
    mean = tot[0:1]
    rstd = lax.rsqrt(tot[1:2] - mean * mean + EPS)
    loads[0, "v"].wait()
    loads[1, "v"].wait()
    gam = vec[0]
    bet = vec[1]
    ngain = rstd * gam

    SB = 32

    def gate(r, p):
        am = abuf[r, p:p + SB, :].astype(F32) - mean
        n = am * ngain + bet
        n2 = n * n
        th = jnp.tanh(n * (n2 * (GC0 * GC1) + GC0))
        return am, n, n2, 0.5 * th + 0.5

    def z_row(r):
        first = last = None
        for i in range(TW // SB):
            p = i * SB
            am, n, n2, hp = gate(r, p)
            z = n * hp
            uz[r + 1, TB + p:TB + p + SB, :] = z.astype(BF16)
            if i == 0:
                first = z[0:TB]
            if i == TW // SB - 1:
                last = z[SB - TB:SB]
        pad_blocks(2, uz, r, first, last)

    def convt2_z(k, _):
        with jax.named_scope("convt2z"):
            for i in range(8):
                z_row((k - 4) * 8 + i)
            convt2(k)
        return 0
    lax.fori_loop(4, 8, convt2_z, 0)
    with jax.named_scope("hstart"):
        halo_start(2, uz)

    def dn_row(r, carry):
        t0, t1 = carry
        for i in range(TW // SB):
            p = i * SB
            am, n, n2, hp = gate(r, p)
            dg = hp + n * ((hp - hp * hp) * (n2 * (6.0 * GC0 * GC1) + 2.0 * GC0))
            dn = dz[r, p:p + SB, :] * dg
            dz[r, p:p + SB, :] = dn
            t0 = t0 + _fold8(dn * am)
            t1 = t1 + _fold8(dn)
        return t0, t1

    raw[...] = jnp.zeros((C, C), F32)

    def wgrad2_dn(t, carry):
        @pl.when(t == 1)
        def _():
            with jax.named_scope("hrow_z"):
                halo_row(2, uz)

        @pl.when(t == 3)
        def _():
            with jax.named_scope("hcol_z"):
                halo_cols(2, uz)
        with jax.named_scope("tap2dn"):
            for i in range(8):
                carry = dn_row(t * 8 + i, carry)
            tap(0, uz, gn, t)
        return carry
    t0, t1 = lax.fori_loop(0, 4, wgrad2_dn, (zero, zero))
    with jax.named_scope("ststart"):
        stat_start(1, t0.sum(0, keepdims=True) * rstd, t1.sum(0, keepdims=True))

    def wgrad2_plain(t, _):
        sums_at(0, 4, 7, t)
        with jax.named_scope("tap2"):
            tap(0, uz, gn, t)
        return 0
    lax.fori_loop(4, 7, wgrad2_plain, 0)

    with jax.named_scope("stat1"):
        tot = stat_finish(1)
    vec[2] = tot[0:1]
    vec[3] = tot[1:2]
    outv = [pltpu.make_async_copy(vec.at[2 + q], (dgam_hbm, dbet_hbm)[q], vec_sem.at[q]) for q in range(2)]
    for cp in outv:
        cp.start()
    us = _group_sum(tot * gam) / CNT
    k0 = rstd * gam
    k1 = rstd * rstd * us[0:1]
    k2 = rstd * us[1:2]

    def da_row(r):
        first = last = None
        for i in range(TW // SB):
            p = i * SB
            am = abuf[r, p:p + SB, :].astype(F32) - mean
            d = dz[r, p:p + SB, :] * k0 - (am * k1 + k2)
            ud[r + 1, TB + p:TB + p + SB, :] = d.astype(BF16)
            if i == 0:
                first = d[0:TB]
            if i == TW // SB - 1:
                last = d[SB - TB:SB]
        pad_blocks(3, ud, r, first, last)
        xn[r] = ud[r + 1, TB:TB + TW, :].T

    def wgrad2_da(t, _):
        sums_at(0, 7, 9, t)
        with jax.named_scope("tap2da"):
            for i in range(16):
                da_row((t - 7) * 16 + i)
            tap(0, uz, gn, t)
        return 0
    lax.fori_loop(7, 9, wgrad2_da, 0)
    with jax.named_scope("hstart"):
        halo_start(3, ud)
    turn(0, 8)

    def wgrad1_step(t, _):
        sums_at(9, 0, 9, t)
        with jax.named_scope("tap1"):
            tap(1, ux, xn, t)
        return 0
    lax.fori_loop(0, 9, wgrad1_step, 0)
    turn(1, 8)
    with jax.named_scope("hfin_d"):
        halo_row(3, ud)
        halo_cols(3, ud)

    def out_copy(q, k):
        src, dst = ((abuf, y_hbm), (ost, dx_hbm))[q]
        return pltpu.make_async_copy(src.at[pl.ds(k * R, R)], dst.at[pl.ds(k * R, R)], out_sem.at[q, k])

    def out_step(q, u, wt, res, out, k):
        acc = conv(u, wt, k * R).reshape(R, TW, C)
        v = acc + res[pl.ds(k * R + 1, R), TB:TB + TW, :].astype(F32)
        out[pl.ds(k * R, R)] = v.astype(BF16)
        out_copy(q, k).start()

    def y_step(k, _):
        sums_at(26, 0, 8, k)
        with jax.named_scope("y"):
            out_step(0, uz, w2, ux, abuf, k)
        return 0

    def dx_step(k, _):
        sums_at(18, 0, 8, k)
        with jax.named_scope("dx"):
            out_step(1, ud, w1t, ug, ost, k)
        return 0
    lax.fori_loop(0, TH // R, dx_step, 0)
    lax.fori_loop(0, TH // R, y_step, 0)
    for sl in range(34, 40):
        for n, c, k in plan_at.get(sl, ()):
            ar_step(n, c, k)
    with jax.named_scope("outw"):
        for q in range(2):
            outv[q].wait()
            for k in range(TH // R):
                out_copy(q, k).wait()


def finish(y_ref, dx_ref, w1_ref, w2_ref, ga_ref, be_ref, yo, dxo, w1o, w2o, gao, beo, qm):
    qi = lax.broadcasted_iota(jnp.int32, (TW, TW), 0)
    qj = lax.broadcasted_iota(jnp.int32, (TW, TW), 1)

    @pl.when(pl.program_id(0) == 0)
    def _():
        qm[...] = jnp.where(qi == (qj & 15) * TB + (qj >> 4), 1.0, 0.0).astype(BF16)
    for src, dst in ((y_ref, yo), (dx_ref, dxo)):
        for r in range(src.shape[0]):
            dst[r] = jnp.dot(qm[...], src[r], preferred_element_type=F32).astype(BF16)
    w1o[...] = w1_ref[...]
    w2o[...] = w2_ref[...]
    gao[...] = ga_ref[...]
    beo[...] = be_ref[...]


def solution(mesh):
    tile = P(None, 'h', 'w', None)

    def body(x, w1, gamma, beta, w2, g):
        anyspec = pl.BlockSpec(memory_space=pl.ANY)
        S = jax.ShapeDtypeStruct
        V = pltpu.VMEM
        DMA = pltpu.SemaphoreType.DMA
        img = (TH, TW, C)
        uimg = (TH + 2, EXT, C)
        out = pl.pallas_call(
            kernel,
            out_shape=(S(img, BF16), S(img, BF16), S((3, 3, C, C), F32), S((3, 3, C, C), F32), S((1, C), F32), S((1, C), F32)),
            in_specs=[anyspec] * 6,
            out_specs=(anyspec,) * 6,
            scratch_shapes=[
                V(img, BF16), V(img, BF16), V(uimg, BF16), V(uimg, BF16), V(uimg, BF16), V(uimg, BF16),
                V(img, BF16), V(img, BF16), V(img, F32), V((C, C), F32),
                V((9 * C, C), BF16), V((9 * C, C), BF16), V((9 * C, C), BF16), V((9 * C, C), BF16),
                V((2, 3, 3, C, C), F32), V((2, 3, 3, 128, C), F32), V((2, 3, 2, 3, 32, C), F32), V((2, 3, 2, 3, 16, C), F32),
                V((4, 2, TH, C), F32), V((4, 2, TH, C), F32), V((4, 2, 8, C), F32), V((2, ND, 8, C), F32),
                V((EXT, TW), BF16), V((4, 1, C), F32),
                DMA((2 * NX + 2,)), DMA((2,)), DMA((2, TH // R)), DMA((4, 5)), DMA((4, 5)), DMA((2, ND)), DMA((2, ND)), DMA((2, 3, 10)), DMA((2, 3, 10)),
            ],
            compiler_params=pltpu.CompilerParams(collective_id=0, has_side_effects=True, vmem_limit_bytes=67043328),
        )(x.reshape(img), w1.reshape(9 * C, C), gamma.reshape(1, C), beta.reshape(1, C), w2.reshape(9 * C, C), g.reshape(img))
        y, dx, dw1, dw2, dgam, dbet = out
        steps = 8
        wrows = (9 * C, C)
        ispec = pl.BlockSpec((TH // steps, TW, C), lambda i: (i, 0, 0))
        wspec = pl.BlockSpec((9 * C // steps, C), lambda i: (i, 0))
        cspec = pl.BlockSpec((1, C), lambda i: (0, 0))
        y, dx, dw1, dw2, dgam, dbet = pl.pallas_call(
            finish,
            grid=(steps,),
            out_shape=(S(img, BF16), S(img, BF16), S(wrows, F32), S(wrows, F32), S((1, C), F32), S((1, C), F32)),
            in_specs=[ispec, ispec, wspec, wspec, cspec, cspec],
            out_specs=(ispec, ispec, wspec, wspec, cspec, cspec),
            scratch_shapes=[V((TW, TW), BF16)],
        )(y, dx, dw1.reshape(wrows), dw2.reshape(wrows), dgam, dbet)
        return (y.reshape(x.shape), dx.reshape(x.shape), dw1.reshape(w1.shape), dw2.reshape(w2.shape), dgam.reshape(C), dbet.reshape(C))

    return jax.shard_map(body, mesh=mesh, in_specs=(tile, P(), P(), P(), P(), tile), out_specs=(tile, tile, P(), P(), P(), P()), check_vma=False)
```

time: 136 us -> 107 us (0.79)
  Pallas kernels: 122 us -> 106 us
  local copies, waits for them, and re-layouts: 13 us -> 0 us
    pallas_call x1 -> x2, Pallas kernels: 122 us -> 106 us  [the longest x1 93.6 us: body(): pl.pallas_call(kernel, out_shape=(S(img, BF16), S(img, BF16), S((3, 3, C,...]
    unnamed x16 -> x0, local copies, waits for them, and re-layouts: 13 us -> none
where the time goes in v2:
time: 107 us
  Pallas kernels  106 us (99%)
    pallas_call x1, Pallas kernels, body(): pl.pallas_call(kernel, out_shape=(S(img, BF16), S(img, BF16), S((3, 3, C,...  93.6 us
    pallas_call x1, Pallas kernels, body(): pl.pallas_call(finish, grid=(steps,), out_shape=(S(img, BF16), S(img, BF1...  12.2 us

profile of v2, /device:TPU:0, one launch (start us, length us, event | category | flops | bytes accessed | tf_op | source)
XLA Modules:
  0.0 106.6 jit_solution(1481469251998604000)
XLA Ops:
  0.6 93.6 %shard_map.109 = (bf16[32,256,256]{2,1,0:T(8,128)(2,1)}, bf16[32,256,256]{2,1,0:T(8,128)(2,1)}, f32[3,3,256,256]{3,2,1,0:T(8,128)}, f32[3,3,256,256]{3,2,1,0:T(8...) custom-call(bf16[32,256,256]{2,1,0:T(8,128)(2,1)} %bitcast.14, bf16[2304,256]{1,0:T(8,128)(2,1)} %bitcast.18, ...), custom_call_target="tpu_custom_call" | custom-call | tf_op jit(solution)/shard_map/pallas_call | solution.py:537
  94.2 12.2 %shard_map.110 = (bf16[32,256,256]{2,1,0:T(8,128)(2,1)}, bf16[32,256,256]{2,1,0:T(8,128)(2,1)}, f32[2304,256]{1,0:T(8,128)}, f32[2304,256]{1,0:T(8,128)}, f32[1,256]{1,0:T(1,128)}, /*index=5*/f32[1,256]{1,0:T(1,128)}) custom-call(bf16[32,256,256]{2,1,0:T(8,128)(2,1)} %get-tuple-element.18.y_ref, bf16[32,256,256]{2,1,0:T(8,128)(2,1)} %get-tuple-element.19.dx_ref, ...), custom_call_target="tpu_custom_call" | custom-call | tf_op jit(solution)/shard_map/pallas_call | solution.py:559

commit v3 on v2

--- a/solution.py
+++ b/solution.py
@@ -34,6 +34,17 @@
     return v
 
 
+def _loop(lo, hi, f):
+    def body(i, c):
+        f(i)
+        return c
+    lax.fori_loop(lo, hi, body, 0)
+
+
+def _row(v):
+    return v.sum(0, keepdims=True)
+
+
 def _fold8(v):
     return v.reshape(v.shape[0] // 8, 8, C).sum(0)
 
@@ -69,21 +80,15 @@
 
     pi = lax.broadcasted_iota(jnp.int32, (EXT, TW), 0)
     pj = lax.broadcasted_iota(jnp.int32, (EXT, TW), 1)
-    pm[...] = jnp.where(pj == (pi & 15) * TB + (pi >> 4) - 1, 1.0, 0.0).astype(BF16)
+    pm[:, :] = jnp.where(pj == (pi & 15) * TB + (pi >> 4) - 1, 1.0, 0.0).astype(BF16)
     for u in (ux, ug, uz, ud):
         u[pl.ds(33 * h, 1)] = jnp.zeros((1, EXT, C), BF16)
 
-    @pl.when(w == 0)
-    def _():
-        for q in range(4):
-            cr[q, 0] = jnp.zeros((TH, C), F32)
-            cc[q, 0] = jnp.zeros((8, C), F32)
-
-    @pl.when(w == NW - 1)
-    def _():
-        for q in range(4):
-            cr[q, 1] = jnp.zeros((TH, C), F32)
-            cc[q, 1] = jnp.zeros((8, C), F32)
+    def no_neighbour(side):
+        cr[:, side] = jnp.zeros((4, TH, C), F32)
+        cc[:, side] = jnp.zeros((4, 8, C), F32)
+    pl.when(w == 0)(lambda: no_neighbour(0))
+    pl.when(w == NW - 1)(lambda: no_neighbour(1))
 
     def to_dev(dw_, dh):
         return {"w": w + dw_, "h": h if dh == 0 else 1 - h}
@@ -101,9 +106,10 @@
         right = [make(3, cs.at[q, 1], cr.at[q, 0], to_dev(1, 0)), make(4, cs.at[q, 1, slab], cc.at[q, 0], to_dev(1, 1))]
         return row, left, right
 
-    def halo_start(q, u):
+    def halo_start(q, u, row_too=True):
         row, left, right = halo_copies(q, u)
-        row().start()
+        if row_too:
+            row().start()
 
         @pl.when(w > 0)
         def _():
@@ -118,10 +124,10 @@
     sub = lax.broadcasted_iota(jnp.int32, (TB, C), 0)
 
     def put(u, r, lo, hi):
-        b0 = u[r, 0:TB, :].astype(F32)
-        u[r, 0:TB, :] = jnp.where(sub == 0, lo, b0).astype(BF16)
-        b1 = u[r, TW + TB:EXT, :].astype(F32)
-        u[r, TW + TB:EXT, :] = jnp.where(sub == TB - 1, hi, b1).astype(BF16)
+        b0 = u[r, :TB, :].astype(F32)
+        u[r, :TB, :] = jnp.where(sub == 0, lo, b0).astype(BF16)
+        b1 = u[r, TW + TB:, :].astype(F32)
+        u[r, TW + TB:, :] = jnp.where(sub == TB - 1, hi, b1).astype(BF16)
 
     def halo_row(q, u):
         halo_copies(q, u)[0]().wait()
@@ -143,43 +149,43 @@
             for cp in left:
                 cp().wait_recv()
 
-        def step(k, _):
+        def step(k):
             for i in range(4):
                 r = k * 4 + i
                 put(u, r + 1, cr[q, 0, pl.ds(r, 1), :], cr[q, 1, pl.ds(r, 1), :])
-            return 0
-        lax.fori_loop(0, TH // 4, step, 0)
+        _loop(0, TH // 4, step)
         put(u, 33 * (1 - h), cc[q, 0, pl.ds(7 * h, 1), :], cc[q, 1, pl.ds(7 * h, 1), :])
 
     def permute_in(q, src, u):
         for k in range(NX):
-            loads[q, k].wait()
-
-            def step(i, _):
+            if q == 1:
+                loads[q, k].wait()
+
+            def step(i):
                 for d in range(16):
                     r = k * rows + i * 16 + d
-                    v = jnp.dot(pm[...], src[r], preferred_element_type=F32)
+                    v = jnp.dot(pm[:, :], src[r], preferred_element_type=F32)
                     u[r + 1] = v.astype(BF16)
-                    cs[q, 0, pl.ds(r, 1), :] = v[TB:TB + 1]
-                    cs[q, 1, pl.ds(r, 1), :] = v[TW + TB - 1:TW + TB]
-                return 0
-            lax.fori_loop(0, rows // 16, step, 0)
+                    if q == 1:
+                        cs[q, 0, pl.ds(r, 1), :] = v[TB:TB + 1]
+                        cs[q, 1, pl.ds(r, 1), :] = v[TW + TB - 1:TW + TB]
+            _loop(0, rows // 16, step)
 
     def pad_blocks(q, u, r, first, last):
-        u[r + 1, 0:TB, :] = jnp.where(sub == 0, 0.0, pltpu.roll(last, 1, 0)).astype(BF16)
-        u[r + 1, TW + TB:EXT, :] = jnp.where(sub == TB - 1, 0.0, pltpu.roll(first, TB - 1, 0)).astype(BF16)
+        u[r + 1, :TB, :] = jnp.where(sub == 0, 0.0, pltpu.roll(last, 1, 0)).astype(BF16)
+        u[r + 1, TW + TB:, :] = jnp.where(sub == TB - 1, 0.0, pltpu.roll(first, TB - 1, 0)).astype(BF16)
         cs[q, 0, pl.ds(r, 1), :] = first[0:1]
         cs[q, 1, pl.ds(r, 1), :] = last[TB - 1:TB]
 
     def conv(u, wt, r0, R=R):
         lhs = jnp.concatenate([u[pl.ds(r0 + a, R), TB * b:TB * b + TW, :].reshape(R * TW, C) for a in range(3) for b in range(3)], axis=1)
-        return jnp.dot(lhs, wt[...], preferred_element_type=F32)
+        return jnp.dot(lhs, wt[:, :], preferred_element_type=F32)
 
     def stat_copies(q):
         out = []
         for k in range(1, ND):
             t = lax.rem(me + k, ND)
-            out.append(rcopy(stat.at[q, me], stat.at[q, me], st_send.at[q, k], st_recv.at[q, me], {"w": t // NH, "h": lax.rem(t, NH)}))
+            out.append(rcopy(stat.at[q, me], stat.at[q, me], st_send.at[q], st_recv.at[q], {"w": t // NH, "h": lax.rem(t, NH)}))
         return out
 
     def stat_start(q, a, b):
@@ -188,11 +194,8 @@
             cp.start()
 
     def stat_finish(q):
-        for k in range(1, ND):
-            t = lax.rem(me + k, ND)
-            rcopy(stat.at[q, t], stat.at[q, t], st_send.at[q, k], st_recv.at[q, t], {"w": t // NH, "h": lax.rem(t, NH)}).wait_recv()
-        for cp in stat_copies(q):
-            cp.wait_send()
+        others = stat.at[q, pl.ds(0, ND - 1)]
+        rcopy(others, others, st_send.at[q], st_recv.at[q], dev_c).wait()
         tot = stat[q, 0]
         for k in range(1, ND):
             tot = tot + stat[q, k]
@@ -232,7 +235,7 @@
 
         def make(k):
             src, dst, dev = plan[k]
-            return lambda: rcopy(src, dst, ar_send.at[n, c, k], ar_recv.at[n, c, k], dev)
+            return lambda: rcopy(src, dst, ar_send.at[n, c, k % 2], ar_recv.at[n, c, k], dev)
         return [make(k) for k in range(10)] + [lambda: pltpu.make_async_copy(rd.at[n, c], out, in_sem.at[n * 3 + c])]
 
     AR_SETS = ((0,), (1, 2), (3, 4), (5, 6), (7, 8), (9, 10))
@@ -264,13 +267,10 @@
                 for i in AR_SETS[k]:
                     cps[i]().start()
 
-    LAG = (0, 1, 5, 9, 12, 16, 18)
-    START = (4, 7, 9, 13, 16, 18)
-    SLOTS = {(i // 3, i % 3): [min(s_ + l_, 34) for l_ in LAG] for i, s_ in enumerate(START)}
+    SLOTS = "347:?FI79<?CKQ:;>AHNQ@BGJMQRCEILNQREFILORR"
     plan_at = {}
-    for (n_, c_), at_ in SLOTS.items():
-        for k_, s_ in enumerate(at_):
-            plan_at.setdefault(s_, []).append((n_, c_, k_))
+    for i_, ch_ in enumerate(SLOTS):
+        plan_at.setdefault(ord(ch_) - ord("0"), []).append((i_ // 21, i_ // 7 % 3, i_ % 7))
 
     def sums_at(base, lo, hi, i):
         for sl in range(lo, hi):
@@ -284,41 +284,48 @@
         return (3 * i * i - 5 * i + 2) // 2
 
     def turn(n, t):
-        dw[n, t // 3, perm3(lax.rem(t, 3))] = raw[...].T
-
-    def tap(n, u, vt, t):
-        turn(n, lax.max(t - 1, 0))
-        a = perm3(lax.rem(t, 3))
-        b = perm3(t // 3)
-        rhs = u[pl.ds(a, TH), pl.ds(pl.multiple_of(TB * b, TB), TW), :].reshape(TH * TW, C)
+        dw[n, t // 3, perm3(t % 3)] = raw[:, :].T
+
+    def tap(n, u, vt, t, first):
+        turn(n, lax.max(t - 1, first))
+        rhs = u[pl.ds(perm3(t % 3), TH), pl.ds(pl.multiple_of(TB * perm3(t // 3), TB), TW), :].reshape(TH * TW, C)
         lhs = jnp.concatenate([vt[r] for r in range(TH)], axis=1)
-        raw[...] = jnp.dot(lhs, rhs, preferred_element_type=F32)
-
+        raw[:, :] = jnp.dot(lhs, rhs, preferred_element_type=F32)
+
+    def x_edges(i):
+        for d in range(8):
+            r = i * 8 + d
+            cs[0, 0, pl.ds(r, 1), :] = xn[r, :TB, :].astype(F32)[:1]
+            cs[0, 1, pl.ds(r, 1), :] = xn[r, TW - TB:, :].astype(F32)[TB - 1:]
+    with jax.named_scope("edges"):
+        for k in range(NX):
+            loads[0, k].wait()
+        _loop(0, TH // 8, x_edges)
     with jax.named_scope("barrier"):
         pl.semaphore_wait(barrier, ND - 1)
+    halo_start(0, ux, False)
     with jax.named_scope("perm_x"):
         permute_in(0, xn, ux)
-    with jax.named_scope("hstart"):
-        halo_start(0, ux)
+    halo_copies(0, ux)[0]().start()
     with jax.named_scope("perm_g"):
         permute_in(1, gn, ug)
-    with jax.named_scope("hstart"):
-        halo_start(1, ug)
+    halo_start(1, ug)
     loads[0, "w"].wait()
     loads[1, "w"].wait()
-
-    def wtrans(t, _):
-        w1t[pl.ds(pl.multiple_of((8 - t) * C, C), C), :] = w1[pl.ds(pl.multiple_of(t * C, C), C), :].T
-        w2t[pl.ds(pl.multiple_of((8 - t) * C, C), C), :] = w2[pl.ds(pl.multiple_of(t * C, C), C), :].T
-        return 0
-    with jax.named_scope("wtrans"):
-        lax.fori_loop(0, 9, wtrans, 0)
     with jax.named_scope("hfin_x"):
         halo_row(0, ux)
         halo_cols(0, ux)
 
+    def wtrans(k):
+        for i in range(3):
+            t = lax.min(k * 3 + i, 8)
+            src, dst = pl.ds(pl.multiple_of(t * C, C), C), pl.ds(pl.multiple_of((8 - t) * C, C), C)
+            w1t[dst, :] = w1[src, :].T
+            w2t[dst, :] = w2[src, :].T
+
     def conv1_step(k, carry):
         s1, s2 = carry
+        wtrans(k)
         a = conv(ux, w1, k * 8, 8).astype(BF16)
         abuf[pl.ds(k * 8, 8)] = a.reshape(8, TW, C)
         af = a.astype(F32)
@@ -327,7 +334,7 @@
     with jax.named_scope("conv1"):
         s1, s2 = lax.fori_loop(0, TH // 8, conv1_step, (zero, zero))
     with jax.named_scope("ststart"):
-        stat_start(0, s1.sum(0, keepdims=True), s2.sum(0, keepdims=True))
+        stat_start(0, _row(s1), _row(s2))
     with jax.named_scope("hfin_g"):
         halo_row(1, ug)
         halo_cols(1, ug)
@@ -338,11 +345,10 @@
             r = k * R + i
             gn[r] = ug[r + 1, TB:TB + TW, :].T
 
-    def convt2_first(k, _):
+    def convt2_first(k):
         convt2(k)
-        return 0
     with jax.named_scope("convt2"):
-        lax.fori_loop(0, 4, convt2_first, 0)
+        _loop(0, 4, convt2_first)
 
     with jax.named_scope("stat0"):
         tot = _group_sum(stat_finish(0)) / CNT
@@ -356,75 +362,90 @@
 
     SB = 32
 
-    def gate(r, p):
-        am = abuf[r, p:p + SB, :].astype(F32) - mean
+    def gate(r, sl):
+        am = abuf[r, sl, :].astype(F32) - mean
         n = am * ngain + bet
         n2 = n * n
         th = jnp.tanh(n * (n2 * (GC0 * GC1) + GC0))
         return am, n, n2, 0.5 * th + 0.5
 
-    def z_row(r):
+    def slope(n, n2, hp):
+        return hp + n * ((hp - hp * hp) * (n2 * (6.0 * GC0 * GC1) + 2.0 * GC0))
+
+    def act_row(r, carry, do_z, do_dn):
+        t0, t1 = carry
         first = last = None
         for i in range(TW // SB):
-            p = i * SB
-            am, n, n2, hp = gate(r, p)
-            z = n * hp
-            uz[r + 1, TB + p:TB + p + SB, :] = z.astype(BF16)
-            if i == 0:
-                first = z[0:TB]
-            if i == TW // SB - 1:
-                last = z[SB - TB:SB]
-        pad_blocks(2, uz, r, first, last)
-
-    def convt2_z(k, _):
+            sl = pl.ds(i * SB, SB)
+            am, n, n2, hp = gate(r, sl)
+            if do_z:
+                z = n * hp
+                uz[r + 1, pl.ds(TB + i * SB, SB), :] = z.astype(BF16)
+                first = z[:TB] if first is None else first
+                last = z[SB - TB:]
+            if do_dn:
+                dn = dz[r, sl, :] * slope(n, n2, hp)
+                dz[r, sl, :] = dn
+                t0 = t0 + _fold8(dn * am)
+                t1 = t1 + _fold8(dn)
+        if do_z:
+            pad_blocks(2, uz, r, first, last)
+        return t0, t1
+
+    def convt2_z(k):
         with jax.named_scope("convt2z"):
             for i in range(8):
-                z_row((k - 4) * 8 + i)
+                act_row((k - 4) * 8 + i, (zero, zero), True, False)
             convt2(k)
-        return 0
-    lax.fori_loop(4, 8, convt2_z, 0)
+    _loop(4, 8, convt2_z)
     with jax.named_scope("hstart"):
         halo_start(2, uz)
-
-    def dn_row(r, carry):
-        t0, t1 = carry
-        for i in range(TW // SB):
-            p = i * SB
-            am, n, n2, hp = gate(r, p)
-            dg = hp + n * ((hp - hp * hp) * (n2 * (6.0 * GC0 * GC1) + 2.0 * GC0))
-            dn = dz[r, p:p + SB, :] * dg
-            dz[r, p:p + SB, :] = dn
-            t0 = t0 + _fold8(dn * am)
-            t1 = t1 + _fold8(dn)
-        return t0, t1
-
-    raw[...] = jnp.zeros((C, C), F32)
-
-    def wgrad2_dn(t, carry):
-        @pl.when(t == 1)
-        def _():
-            with jax.named_scope("hrow_z"):
-                halo_row(2, uz)
-
-        @pl.when(t == 3)
-        def _():
-            with jax.named_scope("hcol_z"):
-                halo_cols(2, uz)
-        with jax.named_scope("tap2dn"):
-            for i in range(8):
-                carry = dn_row(t * 8 + i, carry)
-            tap(0, uz, gn, t)
-        return carry
-    t0, t1 = lax.fori_loop(0, 4, wgrad2_dn, (zero, zero))
+    raw[:, :] = jnp.zeros((C, C), F32)
+
+    def tap2(lo, hi, first, rows, carry):
+        def step(t, c):
+            sums_at(0, lo, hi, t)
+            if lo == 0:
+                @pl.when(t == 1)
+                def _():
+                    with jax.named_scope("hrow_z"):
+                        halo_row(2, uz)
+            with jax.named_scope("tap2"):
+                for i in range(rows):
+                    c = act_row((t - lo) * rows + i, c, False, True)
+                tap(0, uz, gn, t, first)
+            return c
+        return lax.fori_loop(lo, hi, step, carry)
+
+    sums = tap2(0, 3, 0, 0, (zero, zero))
+    turn(0, 2)
+    with jax.named_scope("hcol_z"):
+        halo_cols(2, uz)
+    sums = tap2(3, 7, 3, 8, sums)
     with jax.named_scope("ststart"):
-        stat_start(1, t0.sum(0, keepdims=True) * rstd, t1.sum(0, keepdims=True))
-
-    def wgrad2_plain(t, _):
-        sums_at(0, 4, 7, t)
-        with jax.named_scope("tap2"):
-            tap(0, uz, gn, t)
-        return 0
-    lax.fori_loop(4, 7, wgrad2_plain, 0)
+        stat_start(1, _row(sums[0]) * rstd, _row(sums[1]))
+    tap2(7, 9, 3, 0, zero)
+    turn(0, 8)
+
+    def out_copy(q, k):
+        src, dst = (ost if q == 0 else abuf, (y_hbm, dx_hbm)[q])
+        return pltpu.make_async_copy(src.at[pl.ds(k * R, R)], dst.at[pl.ds(k * R, R)], out_sem.at[q])
+
+    def out_step(q, u, wt, res, out, k):
+        acc = conv(u, wt, k * R).reshape(R, TW, C)
+        v = acc + res[pl.ds(k * R + 1, R), TB:TB + TW, :].astype(F32)
+        out[pl.ds(k * R, R)] = v.astype(BF16)
+        out_copy(q, k).start()
+
+    def y_rows(lo, hi, slot, extra=None):
+        def step(k):
+            sums_at(slot - lo, lo, hi, k)
+            with jax.named_scope("y"):
+                if extra is not None:
+                    extra(k)
+                out_step(0, uz, w2, ux, ost, k)
+        _loop(lo, hi, step)
+    y_rows(0, 1, 9)
 
     with jax.named_scope("stat1"):
         tot = stat_finish(1)
@@ -441,71 +462,46 @@
     def da_row(r):
         first = last = None
         for i in range(TW // SB):
-            p = i * SB
-            am = abuf[r, p:p + SB, :].astype(F32) - mean
-            d = dz[r, p:p + SB, :] * k0 - (am * k1 + k2)
-            ud[r + 1, TB + p:TB + p + SB, :] = d.astype(BF16)
-            if i == 0:
-                first = d[0:TB]
-            if i == TW // SB - 1:
-                last = d[SB - TB:SB]
+            sl = pl.ds(i * SB, SB)
+            am = abuf[r, sl, :].astype(F32) - mean
+            d = dz[r, sl, :] * k0 - (am * k1 + k2)
+            ud[r + 1, pl.ds(TB + i * SB, SB), :] = d.astype(BF16)
+            first = d[:TB] if first is None else first
+            last = d[SB - TB:]
         pad_blocks(3, ud, r, first, last)
         xn[r] = ud[r + 1, TB:TB + TW, :].T
 
-    def wgrad2_da(t, _):
-        sums_at(0, 7, 9, t)
-        with jax.named_scope("tap2da"):
-            for i in range(16):
-                da_row((t - 7) * 16 + i)
-            tap(0, uz, gn, t)
-        return 0
-    lax.fori_loop(7, 9, wgrad2_da, 0)
+    def da_rows(k):
+        for i in range(16):
+            da_row((k - 1) * 16 + i)
+    y_rows(1, 3, 10, da_rows)
     with jax.named_scope("hstart"):
         halo_start(3, ud)
-    turn(0, 8)
-
-    def wgrad1_step(t, _):
-        sums_at(9, 0, 9, t)
+
+    def wgrad1_step(t):
+        sums_at(12, 0, 9, t)
         with jax.named_scope("tap1"):
-            tap(1, ux, xn, t)
-        return 0
-    lax.fori_loop(0, 9, wgrad1_step, 0)
+            tap(1, ux, xn, t, 0)
+    _loop(0, 9, wgrad1_step)
     turn(1, 8)
     with jax.named_scope("hfin_d"):
         halo_row(3, ud)
         halo_cols(3, ud)
 
-    def out_copy(q, k):
-        src, dst = ((abuf, y_hbm), (ost, dx_hbm))[q]
-        return pltpu.make_async_copy(src.at[pl.ds(k * R, R)], dst.at[pl.ds(k * R, R)], out_sem.at[q, k])
-
-    def out_step(q, u, wt, res, out, k):
-        acc = conv(u, wt, k * R).reshape(R, TW, C)
-        v = acc + res[pl.ds(k * R + 1, R), TB:TB + TW, :].astype(F32)
-        out[pl.ds(k * R, R)] = v.astype(BF16)
-        out_copy(q, k).start()
-
-    def y_step(k, _):
-        sums_at(26, 0, 8, k)
-        with jax.named_scope("y"):
-            out_step(0, uz, w2, ux, abuf, k)
-        return 0
-
-    def dx_step(k, _):
-        sums_at(18, 0, 8, k)
+    def dx_step(k):
+        sums_at(21, 0, 8, k)
         with jax.named_scope("dx"):
-            out_step(1, ud, w1t, ug, ost, k)
-        return 0
-    lax.fori_loop(0, TH // R, dx_step, 0)
-    lax.fori_loop(0, TH // R, y_step, 0)
-    for sl in range(34, 40):
-        for n, c, k in plan_at.get(sl, ()):
-            ar_step(n, c, k)
+            out_step(1, ud, w1t, ug, abuf, k)
+
+    _loop(0, TH // R, dx_step)
+    y_rows(3, 8, 29)
+    for n, c, k in sorted(plan_at[34], key=lambda e: e[2]):
+        ar_step(n, c, k)
     with jax.named_scope("outw"):
         for q in range(2):
             outv[q].wait()
-            for k in range(TH // R):
-                out_copy(q, k).wait()
+            src, dst = (ost if q == 0 else abuf, (y_hbm, dx_hbm)[q])
+            pltpu.make_async_copy(src, dst, out_sem.at[q]).wait()
 
 
 def finish(y_ref, dx_ref, w1_ref, w2_ref, ga_ref, be_ref, yo, dxo, w1o, w2o, gao, beo, qm):
@@ -514,14 +510,14 @@
 
     @pl.when(pl.program_id(0) == 0)
     def _():
-        qm[...] = jnp.where(qi == (qj & 15) * TB + (qj >> 4), 1.0, 0.0).astype(BF16)
+        qm[:, :] = jnp.where(qi == (qj & 15) * TB + (qj >> 4), 1.0, 0.0).astype(BF16)
     for src, dst in ((y_ref, yo), (dx_ref, dxo)):
         for r in range(src.shape[0]):
-            dst[r] = jnp.dot(qm[...], src[r], preferred_element_type=F32).astype(BF16)
-    w1o[...] = w1_ref[...]
-    w2o[...] = w2_ref[...]
-    gao[...] = ga_ref[...]
-    beo[...] = be_ref[...]
+            dst[r] = jnp.dot(qm[:, :], src[r], preferred_element_type=F32).astype(BF16)
+    w1o[:, :] = w1_ref[:, :]
+    w2o[:, :] = w2_ref[:, :]
+    gao[:, :] = ga_ref[:, :]
+    beo[:, :] = be_ref[:, :]
 
 
 def solution(mesh):
@@ -546,12 +542,12 @@
                 V((2, 3, 3, C, C), F32), V((2, 3, 3, 128, C), F32), V((2, 3, 2, 3, 32, C), F32), V((2, 3, 2, 3, 16, C), F32),
                 V((4, 2, TH, C), F32), V((4, 2, TH, C), F32), V((4, 2, 8, C), F32), V((2, ND, 8, C), F32),
                 V((EXT, TW), BF16), V((4, 1, C), F32),
-                DMA((2 * NX + 2,)), DMA((2,)), DMA((2, TH // R)), DMA((4, 5)), DMA((4, 5)), DMA((2, ND)), DMA((2, ND)), DMA((2, 3, 10)), DMA((2, 3, 10)),
+                DMA((2 * NX + 2,)), DMA((2,)), DMA((2,)), DMA((4, 5)), DMA((4, 5)), DMA((2,)), DMA((2,)), DMA((2, 3, 2)), DMA((2, 3, 10)),
             ],
             compiler_params=pltpu.CompilerParams(collective_id=0, has_side_effects=True, vmem_limit_bytes=67043328),
         )(x.reshape(img), w1.reshape(9 * C, C), gamma.reshape(1, C), beta.reshape(1, C), w2.reshape(9 * C, C), g.reshape(img))
         y, dx, dw1, dw2, dgam, dbet = out
-        steps = 8
+        steps = 2
         wrows = (9 * C, C)
         ispec = pl.BlockSpec((TH // steps, TW, C), lambda i: (i, 0, 0))
         wspec = pl.BlockSpec((9 * C // steps, C), lambda i: (i, 0))

time: 107 us -> 98.5 us (0.921)
  Pallas kernels: 106 us -> 97.7 us
    pallas_call x1, Pallas kernels: 93.6 us -> 88.4 us  [body(): pl.pallas_call(kernel, out_shape=(S(img, BF16), S(img, BF16), S((3, 3, C,...]
    pallas_call x1, Pallas kernels: 12.2 us -> 9.32 us  [body(): pl.pallas_call(finish, grid=(steps,), out_shape=(S(img, BF16), S(img, BF1...]
where the time goes in v3:
time: 98.5 us; the launch traced here: 98.4 us
  Pallas kernels  97.7 us (99%)
    pallas_call x1, Pallas kernels, body(): pl.pallas_call(kernel, out_shape=(S(img, BF16), S(img, BF16), S((3, 3, C,...  88.4 us
    pallas_call x1, Pallas kernels, body(): pl.pallas_call(finish, grid=(steps,), out_shape=(S(img, BF16), S(img, BF1...  9.32 us

profile of v3, /device:TPU:0, one launch (start us, length us, event | category | flops | bytes accessed | tf_op | source)
XLA Modules:
  0.0 98.4 jit_solution(7050654515042178659)
XLA Ops:
  0.6 88.4 %shard_map.109 = (bf16[32,256,256]{2,1,0:T(8,128)(2,1)}, bf16[32,256,256]{2,1,0:T(8,128)(2,1)}, f32[3,3,256,256]{3,2,1,0:T(8,128)}, f32[3,3,256,256]{3,2,1,0:T(8...) custom-call(bf16[32,256,256]{2,1,0:T(8,128)(2,1)} %bitcast.14, bf16[2304,256]{1,0:T(8,128)(2,1)} %bitcast.18, ...), custom_call_target="tpu_custom_call" | custom-call | tf_op jit(solution)/shard_map/pallas_call | solution.py:533
  89.0 9.3 %shard_map.110 = (bf16[32,256,256]{2,1,0:T(8,128)(2,1)}, bf16[32,256,256]{2,1,0:T(8,128)(2,1)}, f32[2304,256]{1,0:T(8,128)}, f32[2304,256]{1,0:T(8,128)}, f32[1,256]{1,0:T(1,128)}, /*index=5*/f32[1,256]{1,0:T(1,128)}) custom-call(bf16[32,256,256]{2,1,0:T(8,128)(2,1)} %get-tuple-element.18.y_ref, bf16[32,256,256]{2,1,0:T(8,128)(2,1)} %get-tuple-element.19.dx_ref, ...), custom_call_target="tpu_custom_call" | custom-call | tf_op jit(solution)/shard_map/pallas_call | solution.py:555

commit v4 on v3

--- a/solution.py
+++ b/solution.py
@@ -267,7 +267,7 @@
                 for i in AR_SETS[k]:
                     cps[i]().start()
 
-    SLOTS = "347:?FI79<?CKQ:;>AHNQ@BGJMQRCEILNQREFILORR"
+    SLOTS = "347:?FI79<@CKQ:;>AHNQ@BGJMQRCEILNRREFILORR"
     plan_at = {}
     for i_, ch_ in enumerate(SLOTS):
         plan_at.setdefault(ord(ch_) - ord("0"), []).append((i_ // 21, i_ // 7 % 3, i_ % 7))
@@ -339,16 +339,13 @@
         halo_row(1, ug)
         halo_cols(1, ug)
 
-    def convt2(k):
-        dz[pl.ds(k * R, R)] = conv(ug, w2t, k * R).reshape(R, TW, C)
+    def convt2(k, R=R):
+        dz[pl.ds(k * R, R)] = conv(ug, w2t, k * R, R).reshape(R, TW, C)
         for i in range(R):
             r = k * R + i
             gn[r] = ug[r + 1, TB:TB + TW, :].T
-
-    def convt2_first(k):
-        convt2(k)
     with jax.named_scope("convt2"):
-        _loop(0, 4, convt2_first)
+        _loop(0, 2, lambda k: convt2(k, 2 * R))
 
     with jax.named_scope("stat0"):
         tot = _group_sum(stat_finish(0)) / CNT
@@ -360,7 +357,7 @@
     bet = vec[1]
     ngain = rstd * gam
 
-    SB = 32
+    SB = TB
 
     def gate(r, sl):
         am = abuf[r, sl, :].astype(F32) - mean
@@ -504,20 +501,34 @@
             pltpu.make_async_copy(src, dst, out_sem.at[q]).wait()
 
 
-def finish(y_ref, dx_ref, w1_ref, w2_ref, ga_ref, be_ref, yo, dxo, w1o, w2o, gao, beo, qm):
+def finish(y_ref, dx_ref, w1_ref, w2_ref, ga_ref, be_ref, yo, dxo, w1o, w2o, gao, beo,
+           yi, dxi, yb, dxb, w1b, w2b, gab, beb, qm, isem, osem):
+    nc = 2
+    n = TH // nc
+    jobs = []
+    for k in range(nc):
+        part = pl.ds(k * n, n)
+        for src, mid, buf, dst in ((dx_ref, dxi, dxb, dxo), (y_ref, yi, yb, yo)):
+            jobs.append((src.at[part], mid.at[part], buf.at[part], dst.at[part]))
+        src, buf, dst = ((w2_ref, w2b, w2o), (w1_ref, w1b, w1o))[k]
+        jobs.append((src, buf, None, dst))
+    jobs += [(ga_ref, gab, None, gao), (be_ref, beb, None, beo)]
+    ins = [pltpu.make_async_copy(src, mid, isem.at[i]) for i, (src, mid, _, _) in enumerate(jobs)]
+    for cp in ins:
+        cp.start()
     qi = lax.broadcasted_iota(jnp.int32, (TW, TW), 0)
     qj = lax.broadcasted_iota(jnp.int32, (TW, TW), 1)
-
-    @pl.when(pl.program_id(0) == 0)
-    def _():
-        qm[:, :] = jnp.where(qi == (qj & 15) * TB + (qj >> 4), 1.0, 0.0).astype(BF16)
-    for src, dst in ((y_ref, yo), (dx_ref, dxo)):
-        for r in range(src.shape[0]):
-            dst[r] = jnp.dot(qm[:, :], src[r], preferred_element_type=F32).astype(BF16)
-    w1o[:, :] = w1_ref[:, :]
-    w2o[:, :] = w2_ref[:, :]
-    gao[:, :] = ga_ref[:, :]
-    beo[:, :] = be_ref[:, :]
+    qm[:, :] = jnp.where(qi == (qj & 15) * TB + (qj >> 4), 1.0, 0.0).astype(BF16)
+    outs = []
+    for i, (_, mid, buf, dst) in enumerate(jobs):
+        ins[i].wait()
+        if buf is not None:
+            for r in range(n):
+                buf[r] = jnp.dot(qm[:, :], mid[r], preferred_element_type=F32).astype(BF16)
+        outs.append(pltpu.make_async_copy(mid if buf is None else buf, dst, osem.at[i]))
+        outs[i].start()
+    for cp in outs:
+        cp.wait()
 
 
 def solution(mesh):
@@ -547,19 +558,17 @@
             compiler_params=pltpu.CompilerParams(collective_id=0, has_side_effects=True, vmem_limit_bytes=67043328),
         )(x.reshape(img), w1.reshape(9 * C, C), gamma.reshape(1, C), beta.reshape(1, C), w2.reshape(9 * C, C), g.reshape(img))
         y, dx, dw1, dw2, dgam, dbet = out
-        steps = 2
-        wrows = (9 * C, C)
-        ispec = pl.BlockSpec((TH // steps, TW, C), lambda i: (i, 0, 0))
-        wspec = pl.BlockSpec((9 * C // steps, C), lambda i: (i, 0))
-        cspec = pl.BlockSpec((1, C), lambda i: (0, 0))
+        wgt = (9 * C, C)
+        row = (1, C)
+        shapes = [S(img, BF16), S(img, BF16), S(wgt, F32), S(wgt, F32), S(row, F32), S(row, F32)]
         y, dx, dw1, dw2, dgam, dbet = pl.pallas_call(
             finish,
-            grid=(steps,),
-            out_shape=(S(img, BF16), S(img, BF16), S(wrows, F32), S(wrows, F32), S((1, C), F32), S((1, C), F32)),
-            in_specs=[ispec, ispec, wspec, wspec, cspec, cspec],
-            out_specs=(ispec, ispec, wspec, wspec, cspec, cspec),
-            scratch_shapes=[V((TW, TW), BF16)],
-        )(y, dx, dw1.reshape(wrows), dw2.reshape(wrows), dgam, dbet)
+            out_shape=tuple(shapes),
+            in_specs=[anyspec] * 6,
+            out_specs=(anyspec,) * 6,
+            scratch_shapes=[V(img, BF16), V(img, BF16)] + [V(o.shape, o.dtype) for o in shapes] + [V((TW, TW), BF16), DMA((8,)), DMA((8,))],
+            compiler_params=pltpu.CompilerParams(vmem_limit_bytes=67043328),
+        )(y, dx, dw1.reshape(wgt), dw2.reshape(wgt), dgam, dbet)
         return (y.reshape(x.shape), dx.reshape(x.shape), dw1.reshape(w1.shape), dw2.reshape(w2.shape), dgam.reshape(C), dbet.reshape(C))
 
     return jax.shard_map(body, mesh=mesh, in_specs=(tile, P(), P(), P(), P(), tile), out_specs=(tile, tile, P(), P(), P(), P()), check_vma=False)

time: 98.5 us -> 97.2 us (0.987)
  Pallas kernels: 97.7 us -> 96.3 us
    pallas_call x1, Pallas kernels: 88.4 us -> 86.9 us  [body(): pl.pallas_call(kernel, out_shape=(S(img, BF16), S(img, BF16), S((3, 3, C,...]
where the time goes in v4:
time: 97.2 us; the launch traced here: 97.1 us
  Pallas kernels  96.3 us (99%)
    pallas_call x1, Pallas kernels, body(): pl.pallas_call(kernel, out_shape=(S(img, BF16), S(img, BF16), S((3, 3, C,...  86.9 us
    pallas_call x1, Pallas kernels, body(): pl.pallas_call(finish, out_shape=tuple(shapes), in_specs=[anyspec] * 6, o...  9.35 us

profile of v4, /device:TPU:0, one launch (start us, length us, event | category | flops | bytes accessed | tf_op | source)
XLA Modules:
  0.0 97.1 jit_solution(14987841398170733272)
XLA Ops:
  0.6 86.9 %shard_map.109 = (bf16[32,256,256]{2,1,0:T(8,128)(2,1)}, bf16[32,256,256]{2,1,0:T(8,128)(2,1)}, f32[3,3,256,256]{3,2,1,0:T(8,128)}, f32[3,3,256,256]{3,2,1,0:T(8...) custom-call(bf16[32,256,256]{2,1,0:T(8,128)(2,1)} %bitcast.14, bf16[2304,256]{1,0:T(8,128)(2,1)} %bitcast.18, ...), custom_call_target="tpu_custom_call" | custom-call | tf_op jit(solution)/shard_map/pallas_call | solution.py:544
  87.6 9.4 %shard_map.110 = (bf16[32,256,256]{2,1,0:T(8,128)(2,1)}, bf16[32,256,256]{2,1,0:T(8,128)(2,1)}, f32[2304,256]{1,0:T(8,128)}, f32[2304,256]{1,0:T(8,128)}, f32[1,256]{1,0:T(1,128)}, /*index=5*/f32[1,256]{1,0:T(1,128)}) custom-call(bf16[32,256,256]{2,1,0:T(8,128)(2,1)} %get-tuple-element.18.y_ref, bf16[32,256,256]{2,1,0:T(8,128)(2,1)} %get-tuple-element.19.dx_ref, ...), custom_call_target="tpu_custom_call" | custom-call | tf_op jit(solution)/shard_map/pallas_call | solution.py:564

commit v5 on v4

--- a/solution.py
+++ b/solution.py
@@ -150,10 +150,10 @@
                 cp().wait_recv()
 
         def step(k):
-            for i in range(4):
-                r = k * 4 + i
+            for i in range(8):
+                r = k * 8 + i
                 put(u, r + 1, cr[q, 0, pl.ds(r, 1), :], cr[q, 1, pl.ds(r, 1), :])
-        _loop(0, TH // 4, step)
+        _loop(0, TH // 8, step)
         put(u, 33 * (1 - h), cc[q, 0, pl.ds(7 * h, 1), :], cc[q, 1, pl.ds(7 * h, 1), :])
 
     def permute_in(q, src, u):
@@ -293,14 +293,14 @@
         raw[:, :] = jnp.dot(lhs, rhs, preferred_element_type=F32)
 
     def x_edges(i):
-        for d in range(8):
-            r = i * 8 + d
+        for d in range(16):
+            r = i * 16 + d
             cs[0, 0, pl.ds(r, 1), :] = xn[r, :TB, :].astype(F32)[:1]
             cs[0, 1, pl.ds(r, 1), :] = xn[r, TW - TB:, :].astype(F32)[TB - 1:]
     with jax.named_scope("edges"):
         for k in range(NX):
             loads[0, k].wait()
-        _loop(0, TH // 8, x_edges)
+        _loop(0, TH // 16, x_edges)
     with jax.named_scope("barrier"):
         pl.semaphore_wait(barrier, ND - 1)
     halo_start(0, ux, False)
@@ -503,15 +503,16 @@
 
 def finish(y_ref, dx_ref, w1_ref, w2_ref, ga_ref, be_ref, yo, dxo, w1o, w2o, gao, beo,
            yi, dxi, yb, dxb, w1b, w2b, gab, beb, qm, isem, osem):
-    nc = 2
+    nc = 4
     n = TH // nc
     jobs = []
     for k in range(nc):
         part = pl.ds(k * n, n)
         for src, mid, buf, dst in ((dx_ref, dxi, dxb, dxo), (y_ref, yi, yb, yo)):
             jobs.append((src.at[part], mid.at[part], buf.at[part], dst.at[part]))
-        src, buf, dst = ((w2_ref, w2b, w2o), (w1_ref, w1b, w1o))[k]
-        jobs.append((src, buf, None, dst))
+        if k < 2:
+            src, buf, dst = ((w2_ref, w2b, w2o), (w1_ref, w1b, w1o))[k]
+            jobs.append((src, buf, None, dst))
     jobs += [(ga_ref, gab, None, gao), (be_ref, beb, None, beo)]
     ins = [pltpu.make_async_copy(src, mid, isem.at[i]) for i, (src, mid, _, _) in enumerate(jobs)]
     for cp in ins:
@@ -566,7 +567,7 @@
             out_shape=tuple(shapes),
             in_specs=[anyspec] * 6,
             out_specs=(anyspec,) * 6,
-            scratch_shapes=[V(img, BF16), V(img, BF16)] + [V(o.shape, o.dtype) for o in shapes] + [V((TW, TW), BF16), DMA((8,)), DMA((8,))],
+            scratch_shapes=[V(img, BF16), V(img, BF16)] + [V(o.shape, o.dtype) for o in shapes] + [V((TW, TW), BF16), DMA((12,)), DMA((12,))],
             compiler_params=pltpu.CompilerParams(vmem_limit_bytes=67043328),
         )(y, dx, dw1.reshape(wgt), dw2.reshape(wgt), dgam, dbet)
         return (y.reshape(x.shape), dx.reshape(x.shape), dw1.reshape(w1.shape), dw2.reshape(w2.shape), dgam.reshape(C), dbet.reshape(C))

time: 97.2 us -> 97.1 us (level)
  no operation moved by 1% of the time
where the time goes in v5:
time: 97.1 us; the launch traced here: 97 us
  Pallas kernels  96.2 us (99%)
    pallas_call x1, Pallas kernels, body(): pl.pallas_call(kernel, out_shape=(S(img, BF16), S(img, BF16), S((3, 3, C,...  87 us
    pallas_call x1, Pallas kernels, body(): pl.pallas_call(finish, out_shape=tuple(shapes), in_specs=[anyspec] * 6, o...  9.11 us

profile of v5, /device:TPU:0, one launch (start us, length us, event | category | flops | bytes accessed | tf_op | source)
XLA Modules:
  0.0 97.0 jit_solution(18403828789737878184)
XLA Ops:
  0.6 87.0 %shard_map.109 = (bf16[32,256,256]{2,1,0:T(8,128)(2,1)}, bf16[32,256,256]{2,1,0:T(8,128)(2,1)}, f32[3,3,256,256]{3,2,1,0:T(8,128)}, f32[3,3,256,256]{3,2,1,0:T(8...) custom-call(bf16[32,256,256]{2,1,0:T(8,128)(2,1)} %bitcast.14, bf16[2304,256]{1,0:T(8,128)(2,1)} %bitcast.18, ...), custom_call_target="tpu_custom_call" | custom-call | tf_op jit(solution)/shard_map/pallas_call | solution.py:545
  87.7 9.1 %shard_map.110 = (bf16[32,256,256]{2,1,0:T(8,128)(2,1)}, bf16[32,256,256]{2,1,0:T(8,128)(2,1)}, f32[2304,256]{1,0:T(8,128)}, f32[2304,256]{1,0:T(8,128)}, f32[1,256]{1,0:T(1,128)}, /*index=5*/f32[1,256]{1,0:T(1,128)}) custom-call(bf16[32,256,256]{2,1,0:T(8,128)(2,1)} %get-tuple-element.18.y_ref, bf16[32,256,256]{2,1,0:T(8,128)(2,1)} %get-tuple-element.19.dx_ref, ...), custom_call_target="tpu_custom_call" | custom-call | tf_op jit(solution)/shard_map/pallas_call | solution.py:565

commit v6 on v5

--- a/solution.py
+++ b/solution.py
@@ -503,7 +503,7 @@
 
 def finish(y_ref, dx_ref, w1_ref, w2_ref, ga_ref, be_ref, yo, dxo, w1o, w2o, gao, beo,
            yi, dxi, yb, dxb, w1b, w2b, gab, beb, qm, isem, osem):
-    nc = 4
+    nc = 8
     n = TH // nc
     jobs = []
     for k in range(nc):
@@ -567,7 +567,7 @@
             out_shape=tuple(shapes),
             in_specs=[anyspec] * 6,
             out_specs=(anyspec,) * 6,
-            scratch_shapes=[V(img, BF16), V(img, BF16)] + [V(o.shape, o.dtype) for o in shapes] + [V((TW, TW), BF16), DMA((12,)), DMA((12,))],
+            scratch_shapes=[V(img, BF16), V(img, BF16)] + [V(o.shape, o.dtype) for o in shapes] + [V((TW, TW), BF16), DMA((20,)), DMA((20,))],
             compiler_params=pltpu.CompilerParams(vmem_limit_bytes=67043328),
         )(y, dx, dw1.reshape(wgt), dw2.reshape(wgt), dgam, dbet)
         return (y.reshape(x.shape), dx.reshape(x.shape), dw1.reshape(w1.shape), dw2.reshape(w2.shape), dgam.reshape(C), dbet.reshape(C))

time: 97.1 us -> 98.2 us (1.011)
  Pallas kernels: 96.2 us -> 97.3 us
    pallas_call x1, Pallas kernels: 9.11 us -> 10.2 us  [body(): pl.pallas_call(finish, out_shape=tuple(shapes), in_specs=[anyspec] * 6, o...]
where the time goes in v6:
time: 98.2 us; the launch traced here: 98.1 us
  Pallas kernels  97.3 us (99%)
    pallas_call x1, Pallas kernels, body(): pl.pallas_call(kernel, out_shape=(S(img, BF16), S(img, BF16), S((3, 3, C,...  87 us
    pallas_call x1, Pallas kernels, body(): pl.pallas_call(finish, out_shape=tuple(shapes), in_specs=[anyspec] * 6, o...  10.2 us

profile of v6, /device:TPU:0, one launch (start us, length us, event | category | flops | bytes accessed | tf_op | source)
XLA Modules:
  0.0 98.1 jit_solution(11312065520946501981)
XLA Ops:
  0.6 87.0 %shard_map.109 = (bf16[32,256,256]{2,1,0:T(8,128)(2,1)}, bf16[32,256,256]{2,1,0:T(8,128)(2,1)}, f32[3,3,256,256]{3,2,1,0:T(8,128)}, f32[3,3,256,256]{3,2,1,0:T(8...) custom-call(bf16[32,256,256]{2,1,0:T(8,128)(2,1)} %bitcast.14, bf16[2304,256]{1,0:T(8,128)(2,1)} %bitcast.18, ...), custom_call_target="tpu_custom_call" | custom-call | tf_op jit(solution)/shard_map/pallas_call | solution.py:545
  87.7 10.2 %shard_map.110 = (bf16[32,256,256]{2,1,0:T(8,128)(2,1)}, bf16[32,256,256]{2,1,0:T(8,128)(2,1)}, f32[2304,256]{1,0:T(8,128)}, f32[2304,256]{1,0:T(8,128)}, f32[1,256]{1,0:T(1,128)}, /*index=5*/f32[1,256]{1,0:T(1,128)}) custom-call(bf16[32,256,256]{2,1,0:T(8,128)(2,1)} %get-tuple-element.18.y_ref, bf16[32,256,256]{2,1,0:T(8,128)(2,1)} %get-tuple-element.19.dx_ref, ...), custom_call_target="tpu_custom_call" | custom-call | tf_op jit(solution)/shard_map/pallas_call | solution.py:565
